TPU v7x, 256 devices: a whole 4x4x8 slice. The times are simulated.
256 devices in a mesh: gz: 16 (over z_hi, y, core), gy: 4 (over z_lo), ta: 4 (over x).
Axes of the slice: x: 4, y: 4, z: 8 (z_hi: 2, z_lo: 4; z = z_hi * 4 + z_lo), core: 2. Of those that a mesh axis runs over, the one named last changes fastest.
Arguments:
- movie: float32 [524288, 512], P(('gz', 'gy'), 'ta'), may hold values from 0 to 2
- traces: float32 [2048, 512], P(('gz', 'gy'), 'ta'), may hold values from 0.1 to 2
- entry_comp: int32 [4096, 8], P(('gz', 'gy')), may hold values from 0 to 2048, as said below
- footprints: float32 [4096, 8, 128], P(('gz', 'gy')), may hold values from 0.05 to 0.5
Outputs:
- traces_out: float32 [2048, 512], P(('gz', 'gy'), 'ta')
- footprints_out: float32 [4096, 8, 128], P(('gz', 'gy'))
Inputs may be any that keep to these rules, and one draw needn't show every extreme that they name: `entry_comp`: the value 2048 marks an empty slot. In every tile the occupied slots come first; a tile holds up to 8 components, some tile holds 8 in every draw, and a component may appear in several tiles and blocks.
All inputs are finite; a program needn't handle non-finite values.
Results may differ from a plain program's by a relative error of at most 0.0001.
Values sent between devices are 32-bit elements; how exact they have to be, the bound alone decides.
No kernel may reach another device: no remote copies, remote signals or barrier semaphores. Data moves between devices by JAX's collectives and lax.ppermute only.
A program may use at most 64 MiB of HBM per device.

v0:
```python
import functools

import jax
import jax.numpy as jnp
from jax import lax
from jax.experimental import pallas as pl
from jax.experimental.pallas import tpu as pltpu
from jax.sharding import Mesh
from jax.sharding import PartitionSpec as P


K = 2048
TILE = 128
SLOTS = 8
ITERS = 2
RIDGE = 1.0
BLOCKS = ("zh", "y", "c", "zl")
NGROUP = 4
GT = 16
UNROLL = 8
HALF = 1024
NBLK = 16
ROWS = 72
WIDE = 264

VM = pl.BlockSpec(memory_space=pltpu.VMEM)
HB = pl.BlockSpec(memory_space=pltpu.HBM)
PARAMS = pltpu.CompilerParams(vmem_limit_bytes=24 * 1024 * 1024)
f32 = jnp.float32
bf16 = jnp.bfloat16


def like(*shape, dtype=f32):
    return jax.ShapeDtypeStruct(shape, dtype)


def cost(macs):
    return pl.CostEstimate(flops=2 * macs, bytes_accessed=1 << 20, transcendentals=0)


def split(x):
    hi = x.astype(bf16)
    lo = (x - hi.astype(f32)).astype(bf16)
    return hi, lo


def nt(a, b):
    return lax.dot_general(a, b, (((1,), (1,)), ((), ())), preferred_element_type=f32)


def nn(a, b):
    return lax.dot_general(a, b, (((1,), (0,)), ((), ())), preferred_element_type=f32)


def nt3(a, b):
    ah, al = split(a)
    bh, bl = split(b)
    return nt(ah, bh) + (nt(ah, bl) + nt(al, bh))


def nn3(a, b):
    ah, al = split(a)
    bh, bl = split(b)
    return nn(ah, bh) + (nn(ah, bl) + nn(al, bh))


def same_tile():
    i = lax.broadcasted_iota(jnp.int32, (128, 128), 0) // SLOTS
    j = lax.broadcasted_iota(jnp.int32, (128, 128), 1) // SLOTS
    return i == j


def stacked(x):
    hi = x.astype(bf16).astype(f32)
    return jnp.concatenate([hi, x - hi], axis=0).astype(bf16)


def as_column(row, n):
    i = lax.broadcasted_iota(jnp.int32, (n, n), 0)
    j = lax.broadcasted_iota(jnp.int32, (n, n), 1)
    return jnp.sum(jnp.where(i == j, row, 0.0), axis=1, keepdims=True)


def project(foot, pair):
    two = stacked(foot)
    out = nn(jnp.concatenate([two, two], axis=1), pair)
    return out[:SLOTS] + out[SLOTS:]


def correlate(picked, pair):
    out = nt(stacked(picked), pair)
    out = out[:SLOTS] + out[SLOTS:]
    return out[:, :TILE] + out[:, TILE:]


def rows_of(g):
    return pl.ds(pl.multiple_of(g * 128, 128), 128)


def first_kernel(
    entry, movie, footprints, place, column, valid, foot, pairs, proj, gram, frames, came, got
):
    zh, y, c, zl = (lax.axis_index(name) for name in BLOCKS)
    x = lax.axis_index("ta")
    tall = GT * TILE
    for k in range(NGROUP):
        g = x ^ k
        at = pl.ds(pl.multiple_of(g * 128, 128), 128)
        pltpu.make_async_copy(footprints.at[at], foot.at[pl.ds(k * 128, 128)], got.at[k]).start()
        at = pl.ds(pl.multiple_of(g * tall, tall), tall)
        pltpu.make_async_copy(movie.at[at], frames.at[pl.ds(k * tall, tall)], came.at[k]).start()
    for k in range(NGROUP):
        s = slice(k * 128, (k + 1) * 128)
        comp = entry[x ^ k]
        owner = comp >> 5
        ozh, oy, oc, ozl = owner >> 5, (owner >> 3) & 3, (owner >> 2) & 1, owner & 3
        block = ((oc ^ c) * 4 + (oy ^ y)) * 4 + (ozl ^ (3 * ozh) ^ zl ^ (3 * zh))
        index = jnp.where(comp < K, block * 64 + (ozh ^ zh) * 32 + (comp & 31), K)
        place[:, s] = index
        at = as_column(index.astype(f32), 128)
        column[s, :] = at.astype(jnp.int32)
        valid[s, :] = jnp.where(at < K, 1.0, 0.0)

    def group(k, carry):
        s = rows_of(k)
        pltpu.make_async_copy(footprints.at[s], foot.at[s], got.at[k]).wait()
        f = foot[s, :] * valid[s, :]
        foot[s, :] = f
        gram[k] = jnp.where(same_tile(), nt3(f, f), 0.0)
        at = pl.ds(pl.multiple_of(k * tall, tall), tall)
        pltpu.make_async_copy(movie.at[at], frames.at[at], came.at[k]).wait()
        parts = []
        for t in range(GT):
            at = pl.ds(pl.multiple_of((k * GT + t) * TILE, TILE), TILE)
            hi, lo = split(frames[at, :])
            pair = jnp.concatenate([hi, lo], axis=0)
            pairs[k * GT + t] = pair
            parts.append(project(f[t * SLOTS : (t + 1) * SLOTS], pair))
        proj[s, :] = jnp.concatenate(parts, axis=0)
        return carry

    lax.fori_loop(0, NGROUP, group, 0)


def first(entry, movie, footprints):
    return pl.pallas_call(
        first_kernel,
        in_specs=[VM, HB, HB],
        out_specs=[VM] * 7,
        out_shape=[
            like(1, 512, dtype=jnp.int32),
            like(512, 1, dtype=jnp.int32),
            like(512, 1),
            like(512, TILE),
            pltpu.VMEM((64, 2 * TILE, 128), bf16),
            like(512, 128),
            like(NGROUP, 128, 128),
        ],
        scratch_shapes=[
            pltpu.VMEM((64 * TILE, 128), f32),
            pltpu.SemaphoreType.DMA((NGROUP,)),
            pltpu.SemaphoreType.DMA((NGROUP,)),
        ],
        compiler_params=PARAMS,
        cost_estimate=cost(64 * 16 * 256 * 128),
        name="first",
    )(
        entry,
        pltpu.with_memory_space_constraint(movie, pltpu.HBM),
        pltpu.with_memory_space_constraint(footprints, pltpu.HBM),
    )


def scatter(half, place, both, curv, out):
    n = place.shape[1]
    lane = lax.broadcasted_iota(jnp.int32, (256, n), 0)
    inside = jnp.where(lane[:128] == place % 64, 1.0, 0.0).astype(bf16)
    block = lax.broadcasted_iota(jnp.int32, (NBLK, n), 0) + half * NBLK
    ch, cl = split(jnp.where(block == place // 64, curv, 0.0))
    den = nt(ch, inside) + nt(cl, inside)
    dens = jnp.concatenate([den, jnp.zeros((8, 128), f32)], axis=0)
    for k in range(4):
        out[k, 256:, :] = dens[k * 4 : k * 4 + 8]

    def block_rows(k, carry):
        hot = jnp.where(lane + (half * HALF + k * 256) == place, 1.0, 0.0).astype(bf16)
        got = nn(hot, both)
        out[k, :256, :] = got[:, :128] + got[:, 128:]
        return carry

    lax.fori_loop(0, 4, block_rows, 0)


def picked_from(half, column, part, add, out):
    both = jnp.concatenate(split(part[...]), axis=1)
    lane = lax.broadcasted_iota(jnp.int32, (256, HALF), 1) + half * HALF

    def some(i, carry):
        s = pl.ds(pl.multiple_of(i * 256, 256), 256)
        hot = jnp.where(lane == column[s, :], 1.0, 0.0).astype(bf16)
        got = nn(hot, both)
        got = got[:, :128] + got[:, 128:]
        out[s, :] = got if add is None else got + add[s, :]
        return carry

    lax.fori_loop(0, 2, some, 0)


def near_kernel(column, near, out):
    picked_from(0, column, near, None, out)


def pick_near(column, near):
    return pl.pallas_call(
        near_kernel,
        in_specs=[VM] * 2,
        out_specs=VM,
        out_shape=like(512, 128),
        compiler_params=PARAMS,
        cost_estimate=cost(512 * HALF * 256),
        name="pick_near",
    )(column, near)


SLOTS_BY_FRAMES = pltpu.VMEM((512, 128), f32)
FAR_OUT = [like(4, WIDE, 128), like(512, 256, dtype=bf16), like(8, 512)]


def scatter_far(place, work, rows, other, both, curv):
    two = jnp.concatenate(split(work[...]), axis=1)
    row = jnp.concatenate(rows, axis=1)
    both[...] = two
    curv[...] = jnp.broadcast_to(row, (8, 512))
    scatter(1, place[...], two, row, other)


def numer_kernel(place, column, proj, gram, got, far, other, both, curv, work):
    picked_from(1, column, far, got, work)
    rows = []
    for g in range(NGROUP):
        s = slice(g * 128, (g + 1) * 128)
        work[s, :] = proj[s, :] - nn3(gram[g], work[s, :])
        rows.append(jnp.sum(gram[g], axis=0, keepdims=True))
    scatter_far(place, work, rows, other, both, curv)


def numerators(place, column, proj, gram, got, far):
    return pl.pallas_call(
        numer_kernel,
        in_specs=[VM] * 6,
        out_specs=[VM] * 3,
        out_shape=FAR_OUT,
        scratch_shapes=[SLOTS_BY_FRAMES],
        compiler_params=PARAMS,
        name="numerators",
    )(place, column, proj, gram, got, far)


def mine_kernel(place, both, curv, mine):
    scatter(0, place[...], both[...], curv[:1, :], mine)


def scatter_mine(place, both, curv):
    return pl.pallas_call(
        mine_kernel,
        in_specs=[VM] * 3,
        out_specs=VM,
        out_shape=like(4, WIDE, 128),
        compiler_params=PARAMS,
        cost_estimate=cost(512 * HALF * 256),
        name="scatter_mine",
    )(place, both, curv)


def fold_core_kernel(mine, came, *outs):
    for k in range(4):
        outs[k][...] = mine[k] + came[k]


def fold_core(mine, came):
    return pl.pallas_call(
        fold_core_kernel,
        in_specs=[VM] * 2,
        out_specs=[VM] * 4,
        out_shape=[like(WIDE, 128)] * 4,
        compiler_params=PARAMS,
        name="fold_core",
    )(mine, came)


def fold_y_kernel(a, b, c, d, *outs):
    den = (a[256:, :] + b[256:, :]) + (c[256:, :] + d[256:, :])
    for k in range(4):
        s = slice(k * 64, (k + 1) * 64)
        outs[k][:64, :] = (a[s, :] + b[s, :]) + (c[s, :] + d[s, :])
        outs[k][64:, :] = jnp.broadcast_to(den[k : k + 1], (8, 128))


def fold_y(parts):
    return pl.pallas_call(
        fold_y_kernel,
        in_specs=[VM] * 4,
        out_specs=[VM] * 4,
        out_shape=[like(ROWS, 128)] * 4,
        compiler_params=PARAMS,
        name="fold_y",
    )(*parts)


def fold_z_kernel(a, b, c, d, out):
    out[...] = (a[...] + b[...]) + (c[...] + d[...])


def fold_z(parts):
    return pl.pallas_call(
        fold_z_kernel,
        in_specs=[VM] * 4,
        out_specs=VM,
        out_shape=like(ROWS, 128),
        compiler_params=PARAMS,
        name="fold_z",
    )(*parts)


def update_kernel(own, came, traces, out):
    a = as_column(own[64:65, :], 128)
    b = as_column(came[64:65, :], 128)
    for h in range(2):
        s = slice(h * 32, (h + 1) * 32)
        o = slice((1 - h) * 32, (2 - h) * 32)
        den = a[s] + b[o] + RIDGE
        out[s, :] = jnp.maximum(traces[s, :] + (own[s, :] + came[o, :]) / den, 0.0)


def update(own, came, traces):
    return pl.pallas_call(
        update_kernel,
        in_specs=[VM] * 3,
        out_specs=VM,
        out_shape=like(64, 128),
        compiler_params=PARAMS,
        name="update",
    )(own, came, traces)


def resident(pairs):
    return pltpu.with_memory_space_constraint(pairs, pltpu.VMEM)


def grad_piece(k, picked, foot, pairs, out):
    p = picked[k * 128 : (k + 1) * 128, :]
    gram = jnp.where(same_tile(), nt3(p, p), 0.0)
    out[128:, :] = jnp.broadcast_to(jnp.sum(gram, axis=0, keepdims=True), (8, 128))
    out[:128, :] = -nn3(gram, foot[k * 128 : (k + 1) * 128, :])

    def tiles(i, carry):
        for j in range(UNROLL):
            t = i * UNROLL + j
            at = pl.ds(pl.multiple_of(k * 128 + t * SLOTS, SLOTS), SLOTS)
            rows = pl.ds(pl.multiple_of(t * SLOTS, SLOTS), SLOTS)
            out[rows, :] += correlate(picked[at, :], pairs[k * GT + t])
        return carry

    lax.fori_loop(0, GT // UNROLL, tiles, 0)


def picked_grad_kernel(k, column, got, far, foot, pairs, picked, out):
    picked_from(1, column, far, got, picked)
    grad_piece(k, picked, foot, pairs, out)


def picked_gradient(k, column, got, far, foot, pairs):
    return pl.pallas_call(
        functools.partial(picked_grad_kernel, k),
        in_specs=[VM] * 5,
        out_specs=[VM] * 2,
        out_shape=[like(512, 128), like(136, 128)],
        compiler_params=PARAMS,
        cost_estimate=cost(512 * HALF * 256),
        name="picked_gradient",
    )(column, got, far, foot, resident(pairs))


def grad_kernel(k, picked, foot, pairs, out):
    grad_piece(k, picked, foot, pairs, out)


def gradient(k, picked, foot, pairs):
    return pl.pallas_call(
        functools.partial(grad_kernel, k),
        in_specs=[VM] * 3,
        out_specs=VM,
        out_shape=like(136, 128),
        compiler_params=PARAMS,
        cost_estimate=cost(16 * 16 * 256 * 128),
        name="gradient",
    )(picked, foot, resident(pairs))


def step_kernel(a, b, c, d, foot, valid, new):
    total = (a[...] + c[...]) + (b[...] + d[...])
    dsp = as_column(total[128:129, :], 128) + RIDGE
    new[...] = jnp.maximum(foot[:128, :] + total[:128] / dsp, 0.0) * valid[:128, :]


def stepped(parts, foot, valid):
    return pl.pallas_call(
        step_kernel,
        in_specs=[VM] * 6,
        out_specs=VM,
        out_shape=like(128, TILE),
        compiler_params=PARAMS,
        name="step",
    )(*parts, foot, valid)


def again_kernel(k, foot, picked, pairs, work, curv):
    f = foot[...]
    gram = jnp.where(same_tile(), nt3(f, f), 0.0)
    curv[...] = jnp.broadcast_to(jnp.sum(gram, axis=0, keepdims=True), (8, 128))
    work[...] = -nn3(gram, picked[k * 128 : (k + 1) * 128, :])

    def tiles(i, carry):
        for j in range(UNROLL):
            t = i * UNROLL + j
            rows = pl.ds(pl.multiple_of(t * SLOTS, SLOTS), SLOTS)
            work[rows, :] += project(foot[rows, :], pairs[k * GT + t])
        return carry

    lax.fori_loop(0, GT // UNROLL, tiles, 0)


def projected(k, foot, picked, pairs):
    return pl.pallas_call(
        functools.partial(again_kernel, k),
        in_specs=[VM] * 3,
        out_specs=[VM] * 2,
        out_shape=[like(128, 128), like(8, 128)],
        compiler_params=PARAMS,
        cost_estimate=cost(16 * 16 * 256 * 128),
        name="projected",
    )(foot, picked, resident(pairs))


def far_kernel(place, w0, w1, w2, w3, c0, c1, c2, c3, other, both, curv, work):
    for k, part in enumerate((w0, w1, w2, w3)):
        work[k * 128 : (k + 1) * 128, :] = part[...]
    scatter_far(place, work, [c[:1, :] for c in (c0, c1, c2, c3)], other, both, curv)


def scatter_other(place, works, curvs):
    return pl.pallas_call(
        far_kernel,
        in_specs=[VM] * 9,
        out_specs=[VM] * 3,
        out_shape=FAR_OUT,
        scratch_shapes=[SLOTS_BY_FRAMES],
        compiler_params=PARAMS,
        name="scatter_other",
    )(place, *works, *curvs)


def last_kernel(f0, f1, f2, f3, new):
    x = lax.axis_index("ta")
    for k, foot in enumerate((f0, f1, f2, f3)):
        new[rows_of(x ^ k), :] = foot[...]


def last(feet):
    return pl.pallas_call(
        last_kernel,
        in_specs=[VM] * 4,
        out_specs=VM,
        out_shape=like(512, TILE),
        compiler_params=PARAMS,
        name="last",
    )(*feet)


def swapped(x, axis, bits):
    n = lax.axis_size(axis)
    return lax.ppermute(x, axis, [(i, i ^ bits) for i in range(n)])


def across(x):
    return swapped(x, ("zh", "zl"), 7)


def summed_blocks(place, other, both, curv):
    came = swapped(other, "c", 1)
    ys = fold_core(scatter_mine(place, both, curv), came)
    zs = fold_y([ys[0]] + [swapped(ys[k], "y", k) for k in (2, 1, 3)])
    own = fold_z([zs[0]] + [swapped(zs[k], "zl", k) for k in (3, 2, 1)])
    return own, across(own)


def gathered(part, axis):
    near = [swapped(part, axis, k) for k in (1, 2, 3)]
    return jnp.concatenate([part] + near, axis=0)


def new_feet(column, near, far, foot, valid, pairs):
    picked, piece = picked_gradient(2, column, pick_near(column, near), far, foot, pairs)
    came = {2: swapped(piece, "ta", 2)}
    for k in (1, 3):
        piece = gradient(k, picked, foot, pairs)
        came[k] = swapped(piece, "ta", k)
    came[0] = gradient(0, picked, foot, pairs)
    own = stepped([came[k] for k in range(NGROUP)], foot, valid)
    return [own] + [swapped(own, "ta", k) for k in (1, 2, 3)], picked


def local(movie, traces, entry_comp, footprints):
    own = jnp.concatenate([traces, across(traces)], axis=0)
    entry = entry_comp.reshape(NGROUP, 1, 128)
    near = gathered(gathered(own, "zl"), "y")
    made = first(entry, movie, footprints.reshape(-1, TILE))
    near, place, column, valid, foot, pairs, proj, gram = lax.optimization_barrier((near, *made))
    far = swapped(near, "c", 1)
    sums = numerators(place, column, proj, gram, pick_near(column, near), far)
    for step in range(ITERS):
        own = update(*summed_blocks(place, *sums), own)
        near = gathered(gathered(own, "zl"), "y")
        far = swapped(near, "c", 1)
        feet, picked = new_feet(column, near, far, foot, valid, pairs)
        if step + 1 < ITERS:
            works, curvs = zip(*(projected(k, feet[k], picked, pairs) for k in range(NGROUP)))
            sums = scatter_other(place, works, curvs)
            foot = jnp.concatenate(feet, axis=0)
    return own[:32], last(feet).reshape(footprints.shape)


def solution(mesh):
    torus = Mesh(
        mesh.devices.reshape(2, 4, 2, mesh.shape["gy"], mesh.shape["ta"]),
        ("zh", "y", "c", "zl", "ta"),
    )
    in_specs = (P(BLOCKS, "ta"), P(BLOCKS, "ta"), P(BLOCKS, None), P(BLOCKS, None, None))
    out_specs = (P(BLOCKS, "ta"), P(BLOCKS, None, None))
    return jax.shard_map(local, mesh=torus, in_specs=in_specs, out_specs=out_specs, check_vma=False)
```

profile of v0, /device:TPU:1, one launch (start us, length us, event | category | flops | bytes accessed | tf_op | source)
XLA Modules:
  0.0 165.6 jit_solution(13586173021675771337)
XLA Ops:
  0.6 6.5 %collective-permute-start = (f32[32,128]{1,0:T(8,128)}, f32[32,128]{1,0:T(8,128)S(1)}, u32[]{:S(2)}, u32[]{:S(2)}) collective-permute-start(f32[32,128]{1,0:T(8,128)} %param.5), channel_id=1, source_target_pairs={{0,140},{4,136},{8,132},{12,128},{128,12},{132,8},{136,4},{140,0},... | collective-permute-start | bytes 49160 | tf_op jit(solution)/shard_map/ppermute | solution.py:482
  11.7 4.0 %collective-permute-done.2 = f32[64,128]{1,0:T(8,128)S(1)} collective-permute-done((f32[64,128]{1,0:T(8,128)S(1)}, f32[64,128]{1,0:T(8,128)S(1)}, u32[]{:S(2)}, u32[]{:S(2)}) %collective-permute-start.2) | collective-permute-done | bytes 32800 | tf_op jit(solution)/shard_map/ppermute | solution.py:482
  17.1 2.6 %collective-permute-start.5 = (f32[256,128]{1,0:T(8,128)S(1)}, f32[256,128]{1,0:T(8,128)S(1)}, u32[]{:S(2)}, u32[]{:S(2)}) collective-permute-start(f32[256,128]{1,0:T(8,128)S(1)} %get-tuple-element.100), channel_id=1, source_target_pairs={{0,64},{32,96},{64,0},{96,32},{1,65},{33,97},{65,1},{97,33},{2,66}... | collective-permute-start | bytes 393224 | tf_op jit(solution)/shard_map/ppermute | solution.py:482
  20.6 3.7 %first.1 = (s32[1,512]{1,0:T(1,128)S(1)}, s32[512,1]{1,0:T(8,128)S(1)}, f32[512,1]{1,0:T(8,128)S(1)}, f32[512,128]{1,0:T(8,128)S(1)}, bf16[64,256,128]{2,1,0:T(8...) custom-call(s32[4,1,128]{2,1,0:T(1,128)S(1)} %bitcast.3, f32[8192,128]{1,0:T(8,128)} %movie.1, ...), custom_call_target="tpu_custom_call" | custom-call | flops 67108864 | bytes 1048576 | tf_op jit(solution)/shard_map/first/pallas_call | solution.py:146
  24.5 5.0 %collective-permute-done.6 = f32[256,128]{1,0:T(8,128)S(1)} collective-permute-done((f32[256,128]{1,0:T(8,128)S(1)}, f32[256,128]{1,0:T(8,128)S(1)}, u32[]{:S(2)}, u32[]{:S(2)}) %collective-permute-start.6) | collective-permute-done | bytes 131104 | tf_op jit(solution)/shard_map/ppermute | solution.py:482
  29.5 4.8 %collective-permute-start.7 = (f32[1024,128]{1,0:T(8,128)S(1)}, f32[1024,128]{1,0:T(8,128)S(1)}, u32[]{:S(2)}, u32[]{:S(2)}) collective-permute-start(f32[1024,128]{1,0:T(8,128)S(1)} %constant_dynamic-update-slice_fusion.7.near), channel_id=1, source_target_pairs={{0,16},{16,0},{1,17},{17,1},{2,18},{18,2},{3,19},{19,3},{4,20},{20... | collective-permute-start | bytes 1572872 | tf_op jit(solution)/shard_map/ppermute | solution.py:482
  35.8 2.1 %numerators.1 = (f32[4,264,128]{2,1,0:T(8,128)S(1)}, bf16[512,256]{1,0:T(8,128)(2,1)S(1)}, f32[8,512]{1,0:T(8,128)S(1)}) custom-call(s32[1,512]{1,0:T(1,128)S(1)} %get-tuple-element.58.place, s32[512,1]{1,0:T(8,128)S(1)} %get-tuple-element.59.column, f32[512,128]{1,0:T(8,128)S(1)} %get-tuple-element.60.proj, f32[4,128,128]{2,1,0:T(8,128)S(1)} %get-tuple-element.61.gram, ...), custom_call_target="tpu_custom_call" | custom-call | tf_op jit(solution)/shard_map/numerators/pallas_call | solution.py:248
  40.6 2.7 %collective-permute-start.11 = (f32[264,128]{1,0:T(8,128)S(1)}, f32[264,128]{1,0:T(8,128)S(1)}, u32[]{:S(2)}, u32[]{:S(2)}) collective-permute-start(f32[264,128]{1,0:T(8,128)S(1)} %get-tuple-element.69), channel_id=1, source_target_pairs={{0,96},{32,64},{64,32},{96,0},{1,97},{33,65},{65,33},{97,1},{2,98}... | collective-permute-start | bytes 405512 | tf_op jit(solution)/shard_map/ppermute | solution.py:482
  43.3 3.1 %collective-permute-done.9.b = f32[264,128]{1,0:T(8,128)S(1)} collective-permute-done((f32[264,128]{1,0:T(8,128)S(1)}, f32[264,128]{1,0:T(8,128)S(1)}, u32[]{:S(2)}, u32[]{:S(2)}) %collective-permute-start.9) | collective-permute-done | bytes 135200 | tf_op jit(solution)/shard_map/ppermute | solution.py:482
  46.8 3.2 %collective-permute-done.11.d = f32[264,128]{1,0:T(8,128)S(1)} collective-permute-done((f32[264,128]{1,0:T(8,128)S(1)}, f32[264,128]{1,0:T(8,128)S(1)}, u32[]{:S(2)}, u32[]{:S(2)}) %collective-permute-start.11) | collective-permute-done | bytes 135200 | tf_op jit(solution)/shard_map/ppermute | solution.py:482
  51.7 2.0 %collective-permute-start.14 = (f32[72,128]{1,0:T(8,128)S(1)}, f32[72,128]{1,0:T(8,128)S(1)}, u32[]{:S(2)}, u32[]{:S(2)}) collective-permute-start(f32[72,128]{1,0:T(8,128)S(1)} %get-tuple-element.73), channel_id=1, source_target_pairs={{0,4},{4,0},{8,12},{12,8},{1,5},{5,1},{9,13},{13,9},{2,6},{6,2},{1... | collective-permute-start | bytes 110600 | tf_op jit(solution)/shard_map/ppermute | solution.py:482
  54.7 2.0 %collective-permute-done.13.c = f32[72,128]{1,0:T(8,128)S(1)} collective-permute-done((f32[72,128]{1,0:T(8,128)S(1)}, f32[72,128]{1,0:T(8,128)S(1)}, u32[]{:S(2)}, u32[]{:S(2)}) %collective-permute-start.13) | collective-permute-done | bytes 36896 | tf_op jit(solution)/shard_map/ppermute | solution.py:482
  56.7 3.6 %collective-permute-start.15 = (f32[72,128]{1,0:T(8,128)S(1)}, f32[72,128]{1,0:T(8,128)S(1)}, u32[]{:S(2)}, u32[]{:S(2)}) collective-permute-start(f32[72,128]{1,0:T(8,128)S(1)} %fold_z.2.own), channel_id=1, source_target_pairs={{0,140},{4,136},{8,132},{12,128},{128,12},{132,8},{136,4},{140,0},... | collective-permute-start | bytes 110600 | tf_op jit(solution)/shard_map/ppermute | solution.py:482
  60.3 1.7 %collective-permute-done.15.came = f32[72,128]{1,0:T(8,128)S(1)} collective-permute-done((f32[72,128]{1,0:T(8,128)S(1)}, f32[72,128]{1,0:T(8,128)S(1)}, u32[]{:S(2)}, u32[]{:S(2)}) %collective-permute-start.15) | collective-permute-done | bytes 36896 | tf_op jit(solution)/shard_map/ppermute | solution.py:482
  62.2 1.8 %collective-permute-start.18 = (f32[64,128]{1,0:T(8,128)S(1)}, f32[64,128]{1,0:T(8,128)S(1)}, u32[]{:S(2)}, u32[]{:S(2)}) collective-permute-start(f32[64,128]{1,0:T(8,128)S(1)} %update.2.traces), channel_id=1, source_target_pairs={{0,12},{4,8},{8,4},{12,0},{1,13},{5,9},{9,5},{13,1},{2,14},{6,10},... | collective-permute-start | bytes 98312 | tf_op jit(solution)/shard_map/ppermute | solution.py:482
  68.2 2.8 %collective-permute-start.19 = (f32[256,128]{1,0:T(8,128)S(1)}, f32[256,128]{1,0:T(8,128)S(1)}, u32[]{:S(2)}, u32[]{:S(2)}) collective-permute-start(f32[256,128]{1,0:T(8,128)S(1)} %pad_maximum_fusion.1), channel_id=1, source_target_pairs={{0,32},{32,0},{64,96},{96,64},{1,33},{33,1},{65,97},{97,65},{2,34}... | collective-permute-start | bytes 393224 | tf_op jit(solution)/shard_map/ppermute | solution.py:482
  71.0 3.7 %collective-permute-done.19 = f32[256,128]{1,0:T(8,128)S(1)} collective-permute-done((f32[256,128]{1,0:T(8,128)S(1)}, f32[256,128]{1,0:T(8,128)S(1)}, u32[]{:S(2)}, u32[]{:S(2)}) %collective-permute-start.19) | collective-permute-done | bytes 131104 | tf_op jit(solution)/shard_map/ppermute | solution.py:482
  74.8 5.6 %collective-permute-start.22 = (f32[1024,128]{1,0:T(8,128)S(1)}, f32[1024,128]{1,0:T(8,128)S(1)}, u32[]{:S(2)}, u32[]{:S(2)}) collective-permute-start(f32[1024,128]{1,0:T(8,128)S(1)} %constant_dynamic-update-slice_fusion.15.near), channel_id=1, source_target_pairs={{0,16},{16,0},{1,17},{17,1},{2,18},{18,2},{3,19},{19,3},{4,20},{20... | collective-permute-start | bytes 1572872 | tf_op jit(solution)/shard_map/ppermute | solution.py:482
  86.6 1.9 %collective-permute-start.25 = (f32[136,128]{1,0:T(8,128)S(1)}, f32[136,128]{1,0:T(8,128)S(1)}, u32[]{:S(2)}, u32[]{:S(2)}) collective-permute-start(f32[136,128]{1,0:T(8,128)S(1)} %gradient.8), channel_id=1, source_target_pairs={{0,3},{1,2},{2,1},{3,0},{4,7},{5,6},{6,5},{7,4},{8,11},{9,10},{10,... | collective-permute-start | bytes 208904 | tf_op jit(solution)/shard_map/ppermute | solution.py:482
  91.0 2.2 %collective-permute-done.24.c = f32[136,128]{1,0:T(8,128)S(1)} collective-permute-done((f32[136,128]{1,0:T(8,128)S(1)}, f32[136,128]{1,0:T(8,128)S(1)}, u32[]{:S(2)}, u32[]{:S(2)}) %collective-permute-start.24) | collective-permute-done | bytes 69664 | tf_op jit(solution)/shard_map/ppermute | solution.py:482
  101.6 3.6 %collective-permute-start.29 = (f32[4,264,128]{2,1,0:T(8,128)S(1)}, f32[4,264,128]{2,1,0:T(8,128)S(1)}, u32[]{:S(2)}, u32[]{:S(2)}) collective-permute-start(f32[4,264,128]{2,1,0:T(8,128)S(1)} %get-tuple-element.89), channel_id=1, source_target_pairs={{0,16},{16,0},{1,17},{17,1},{2,18},{18,2},{3,19},{19,3},{4,20},{20... | collective-permute-start | bytes 1622024 | tf_op jit(solution)/shard_map/ppermute | solution.py:482
  108.5 1.7 %collective-permute-start.32 = (f32[264,128]{1,0:T(8,128)S(1)}, f32[264,128]{1,0:T(8,128)S(1)}, u32[]{:S(2)}, u32[]{:S(2)}) collective-permute-start(f32[264,128]{1,0:T(8,128)S(1)} %get-tuple-element.93), channel_id=1, source_target_pairs={{0,96},{32,64},{64,32},{96,0},{1,97},{33,65},{65,33},{97,1},{2,98}... | collective-permute-start | bytes 405512 | tf_op jit(solution)/shard_map/ppermute | solution.py:482
  110.2 3.0 %collective-permute-done.30.b = f32[264,128]{1,0:T(8,128)S(1)} collective-permute-done((f32[264,128]{1,0:T(8,128)S(1)}, f32[264,128]{1,0:T(8,128)S(1)}, u32[]{:S(2)}, u32[]{:S(2)}) %collective-permute-start.30) | collective-permute-done | bytes 135200 | tf_op jit(solution)/shard_map/ppermute | solution.py:482
  114.7 2.0 %collective-permute-done.32.d = f32[264,128]{1,0:T(8,128)S(1)} collective-permute-done((f32[264,128]{1,0:T(8,128)S(1)}, f32[264,128]{1,0:T(8,128)S(1)}, u32[]{:S(2)}, u32[]{:S(2)}) %collective-permute-start.32) | collective-permute-done | bytes 135200 | tf_op jit(solution)/shard_map/ppermute | solution.py:482
  116.7 1.7 %collective-permute-start.33 = (f32[72,128]{1,0:T(8,128)S(1)}, f32[72,128]{1,0:T(8,128)S(1)}, u32[]{:S(2)}, u32[]{:S(2)}) collective-permute-start(f32[72,128]{1,0:T(8,128)S(1)} %get-tuple-element.95), channel_id=1, source_target_pairs={{0,12},{4,8},{8,4},{12,0},{1,13},{5,9},{9,5},{13,1},{2,14},{6,10},... | collective-permute-start | bytes 110600 | tf_op jit(solution)/shard_map/ppermute | solution.py:482
  118.4 1.9 %collective-permute-start.35 = (f32[72,128]{1,0:T(8,128)S(1)}, f32[72,128]{1,0:T(8,128)S(1)}, u32[]{:S(2)}, u32[]{:S(2)}) collective-permute-start(f32[72,128]{1,0:T(8,128)S(1)} %get-tuple-element.97), channel_id=1, source_target_pairs={{0,4},{4,0},{8,12},{12,8},{1,5},{5,1},{9,13},{13,9},{2,6},{6,2},{1... | collective-permute-start | bytes 110600 | tf_op jit(solution)/shard_map/ppermute | solution.py:482
  123.0 4.0 %collective-permute-start.36 = (f32[72,128]{1,0:T(8,128)S(1)}, f32[72,128]{1,0:T(8,128)S(1)}, u32[]{:S(2)}, u32[]{:S(2)}) collective-permute-start(f32[72,128]{1,0:T(8,128)S(1)} %fold_z.3.own), channel_id=1, source_target_pairs={{0,140},{4,136},{8,132},{12,128},{128,12},{132,8},{136,4},{140,0},... | collective-permute-start | bytes 110600 | tf_op jit(solution)/shard_map/ppermute | solution.py:482
  127.0 1.7 %collective-permute-done.36.came = f32[72,128]{1,0:T(8,128)S(1)} collective-permute-done((f32[72,128]{1,0:T(8,128)S(1)}, f32[72,128]{1,0:T(8,128)S(1)}, u32[]{:S(2)}, u32[]{:S(2)}) %collective-permute-start.36) | collective-permute-done | bytes 36896 | tf_op jit(solution)/shard_map/ppermute | solution.py:482
  134.9 1.9 %collective-permute-start.41 = (f32[256,128]{1,0:T(8,128)S(1)}, f32[256,128]{1,0:T(8,128)S(1)}, u32[]{:S(2)}, u32[]{:S(2)}) collective-permute-start(f32[256,128]{1,0:T(8,128)S(1)} %pad_maximum_fusion.2), channel_id=1, source_target_pairs={{0,64},{32,96},{64,0},{96,32},{1,65},{33,97},{65,1},{97,33},{2,66}... | collective-permute-start | bytes 393224 | tf_op jit(solution)/shard_map/ppermute | solution.py:482
  137.9 3.7 %collective-permute-done.40 = f32[256,128]{1,0:T(8,128)S(1)} collective-permute-done((f32[256,128]{1,0:T(8,128)S(1)}, f32[256,128]{1,0:T(8,128)S(1)}, u32[]{:S(2)}, u32[]{:S(2)}) %collective-permute-start.40) | collective-permute-done | bytes 131104 | tf_op jit(solution)/shard_map/ppermute | solution.py:482
  141.7 5.4 %collective-permute-start.43 = (f32[1024,128]{1,0:T(8,128)S(1)}, f32[1024,128]{1,0:T(8,128)S(1)}, u32[]{:S(2)}, u32[]{:S(2)}) collective-permute-start(f32[1024,128]{1,0:T(8,128)S(1)} %constant_dynamic-update-slice_fusion.22.near), channel_id=1, source_target_pairs={{0,16},{16,0},{1,17},{17,1},{2,18},{18,2},{3,19},{19,3},{4,20},{20... | collective-permute-start | bytes 1572872 | tf_op jit(solution)/shard_map/ppermute | solution.py:482
  157.0 1.9 %collective-permute-done.45.c = f32[136,128]{1,0:T(8,128)S(1)} collective-permute-done((f32[136,128]{1,0:T(8,128)S(1)}, f32[136,128]{1,0:T(8,128)S(1)}, u32[]{:S(2)}, u32[]{:S(2)}) %collective-permute-start.45) | collective-permute-done | bytes 69664 | tf_op jit(solution)/shard_map/ppermute | solution.py:482
  (127 shorter events, 67.1 us)
Async XLA Ops:
  0.6 7.8 %collective-permute-start = (f32[32,128]{1,0:T(8,128)}, f32[32,128]{1,0:T(8,128)S(1)}, u32[]{:S(2)}, u32[]{:S(2)}) collective-permute-start(f32[32,128]{1,0:T(8,128)} %param.5), channel_id=1, source_target_pairs={{0,140},{4,136},{8,132},{12,128},{128,12},{132,8},{136,4},{140,0},... | collective-permute-start | bytes 49160 | tf_op jit(solution)/shard_map/ppermute | solution.py:482
  10.1 5.6 %collective-permute-start.3 = (f32[64,128]{1,0:T(8,128)S(1)}, f32[64,128]{1,0:T(8,128)S(1)}, u32[]{:S(2)}, u32[]{:S(2)}) collective-permute-start(f32[64,128]{1,0:T(8,128)S(1)} %get-tuple-element.108.traces), channel_id=1, source_target_pairs={{0,12},{4,8},{8,4},{12,0},{1,13},{5,9},{9,5},{13,1},{2,14},{6,10},... | collective-permute-start | bytes 98312 | tf_op jit(solution)/shard_map/ppermute | solution.py:482
  15.7 8.7 %collective-permute-start.4 = (f32[256,128]{1,0:T(8,128)S(1)}, f32[256,128]{1,0:T(8,128)S(1)}, u32[]{:S(2)}, u32[]{:S(2)}) collective-permute-start(f32[256,128]{1,0:T(8,128)S(1)} %get-tuple-element.100), channel_id=1, source_target_pairs={{0,32},{32,0},{64,96},{96,64},{1,33},{33,1},{65,97},{97,65},{2,34}... | collective-permute-start | bytes 393224 | tf_op jit(solution)/shard_map/ppermute | solution.py:482
  17.1 7.4 %collective-permute-start.5 = (f32[256,128]{1,0:T(8,128)S(1)}, f32[256,128]{1,0:T(8,128)S(1)}, u32[]{:S(2)}, u32[]{:S(2)}) collective-permute-start(f32[256,128]{1,0:T(8,128)S(1)} %get-tuple-element.100), channel_id=1, source_target_pairs={{0,64},{32,96},{64,0},{96,32},{1,65},{33,97},{65,1},{97,33},{2,66}... | collective-permute-start | bytes 393224 | tf_op jit(solution)/shard_map/ppermute | solution.py:482
  24.3 5.1 %collective-permute-start.6 = (f32[256,128]{1,0:T(8,128)S(1)}, f32[256,128]{1,0:T(8,128)S(1)}, u32[]{:S(2)}, u32[]{:S(2)}) collective-permute-start(f32[256,128]{1,0:T(8,128)S(1)} %get-tuple-element.100), channel_id=1, source_target_pairs={{0,96},{32,64},{64,32},{96,0},{1,97},{33,65},{65,33},{97,1},{2,98}... | collective-permute-start | bytes 393224 | tf_op jit(solution)/shard_map/ppermute | solution.py:482
  29.5 6.4 %collective-permute-start.7 = (f32[1024,128]{1,0:T(8,128)S(1)}, f32[1024,128]{1,0:T(8,128)S(1)}, u32[]{:S(2)}, u32[]{:S(2)}) collective-permute-start(f32[1024,128]{1,0:T(8,128)S(1)} %constant_dynamic-update-slice_fusion.7.near), channel_id=1, source_target_pairs={{0,16},{16,0},{1,17},{17,1},{2,18},{18,2},{3,19},{19,3},{4,20},{20... | collective-permute-start | bytes 1572872 | tf_op jit(solution)/shard_map/ppermute | solution.py:482
  40.0 6.4 %collective-permute-start.9 = (f32[264,128]{1,0:T(8,128)S(1)}, f32[264,128]{1,0:T(8,128)S(1)}, u32[]{:S(2)}, u32[]{:S(2)}) collective-permute-start(f32[264,128]{1,0:T(8,128)S(1)} %get-tuple-element.67), channel_id=1, source_target_pairs={{0,64},{32,96},{64,0},{96,32},{1,65},{33,97},{65,1},{97,33},{2,66}... | collective-permute-start | bytes 405512 | tf_op jit(solution)/shard_map/ppermute | solution.py:482
  40.1 6.7 %collective-permute-start.10 = (f32[264,128]{1,0:T(8,128)S(1)}, f32[264,128]{1,0:T(8,128)S(1)}, u32[]{:S(2)}, u32[]{:S(2)}) collective-permute-start(f32[264,128]{1,0:T(8,128)S(1)} %get-tuple-element.68), channel_id=1, source_target_pairs={{0,32},{32,0},{64,96},{96,64},{1,33},{33,1},{65,97},{97,65},{2,34}... | collective-permute-start | bytes 405512 | tf_op jit(solution)/shard_map/ppermute | solution.py:482
  40.6 9.4 %collective-permute-start.11 = (f32[264,128]{1,0:T(8,128)S(1)}, f32[264,128]{1,0:T(8,128)S(1)}, u32[]{:S(2)}, u32[]{:S(2)}) collective-permute-start(f32[264,128]{1,0:T(8,128)S(1)} %get-tuple-element.69), channel_id=1, source_target_pairs={{0,96},{32,64},{64,32},{96,0},{1,97},{33,65},{65,33},{97,1},{2,98}... | collective-permute-start | bytes 405512 | tf_op jit(solution)/shard_map/ppermute | solution.py:482
  50.0 4.7 %collective-permute-start.12 = (f32[72,128]{1,0:T(8,128)S(1)}, f32[72,128]{1,0:T(8,128)S(1)}, u32[]{:S(2)}, u32[]{:S(2)}) collective-permute-start(f32[72,128]{1,0:T(8,128)S(1)} %get-tuple-element.71), channel_id=1, source_target_pairs={{0,12},{4,8},{8,4},{12,0},{1,13},{5,9},{9,5},{13,1},{2,14},{6,10},... | collective-permute-start | bytes 110600 | tf_op jit(solution)/shard_map/ppermute | solution.py:482
  51.7 5.0 %collective-permute-start.13 = (f32[72,128]{1,0:T(8,128)S(1)}, f32[72,128]{1,0:T(8,128)S(1)}, u32[]{:S(2)}, u32[]{:S(2)}) collective-permute-start(f32[72,128]{1,0:T(8,128)S(1)} %get-tuple-element.72), channel_id=1, source_target_pairs={{0,8},{4,12},{8,0},{12,4},{1,9},{5,13},{9,1},{13,5},{2,10},{6,14},... | collective-permute-start | bytes 110600 | tf_op jit(solution)/shard_map/ppermute | solution.py:482
  51.7 5.0 %collective-permute-start.14 = (f32[72,128]{1,0:T(8,128)S(1)}, f32[72,128]{1,0:T(8,128)S(1)}, u32[]{:S(2)}, u32[]{:S(2)}) collective-permute-start(f32[72,128]{1,0:T(8,128)S(1)} %get-tuple-element.73), channel_id=1, source_target_pairs={{0,4},{4,0},{8,12},{12,8},{1,5},{5,1},{9,13},{13,9},{2,6},{6,2},{1... | collective-permute-start | bytes 110600 | tf_op jit(solution)/shard_map/ppermute | solution.py:482
  56.7 5.4 %collective-permute-start.15 = (f32[72,128]{1,0:T(8,128)S(1)}, f32[72,128]{1,0:T(8,128)S(1)}, u32[]{:S(2)}, u32[]{:S(2)}) collective-permute-start(f32[72,128]{1,0:T(8,128)S(1)} %fold_z.2.own), channel_id=1, source_target_pairs={{0,140},{4,136},{8,132},{12,128},{128,12},{132,8},{136,4},{140,0},... | collective-permute-start | bytes 110600 | tf_op jit(solution)/shard_map/ppermute | solution.py:482
  62.2 4.7 %collective-permute-start.18 = (f32[64,128]{1,0:T(8,128)S(1)}, f32[64,128]{1,0:T(8,128)S(1)}, u32[]{:S(2)}, u32[]{:S(2)}) collective-permute-start(f32[64,128]{1,0:T(8,128)S(1)} %update.2.traces), channel_id=1, source_target_pairs={{0,12},{4,8},{8,4},{12,0},{1,13},{5,9},{9,5},{13,1},{2,14},{6,10},... | collective-permute-start | bytes 98312 | tf_op jit(solution)/shard_map/ppermute | solution.py:482
  67.7 7.1 %collective-permute-start.21 = (f32[256,128]{1,0:T(8,128)S(1)}, f32[256,128]{1,0:T(8,128)S(1)}, u32[]{:S(2)}, u32[]{:S(2)}) collective-permute-start(f32[256,128]{1,0:T(8,128)S(1)} %pad_maximum_fusion.1), channel_id=1, source_target_pairs={{0,96},{32,64},{64,32},{96,0},{1,97},{33,65},{65,33},{97,1},{2,98}... | collective-permute-start | bytes 393224 | tf_op jit(solution)/shard_map/ppermute | solution.py:482
  67.8 7.0 %collective-permute-start.20 = (f32[256,128]{1,0:T(8,128)S(1)}, f32[256,128]{1,0:T(8,128)S(1)}, u32[]{:S(2)}, u32[]{:S(2)}) collective-permute-start(f32[256,128]{1,0:T(8,128)S(1)} %pad_maximum_fusion.1), channel_id=1, source_target_pairs={{0,64},{32,96},{64,0},{96,32},{1,65},{33,97},{65,1},{97,33},{2,66}... | collective-permute-start | bytes 393224 | tf_op jit(solution)/shard_map/ppermute | solution.py:482
  68.2 6.5 %collective-permute-start.19 = (f32[256,128]{1,0:T(8,128)S(1)}, f32[256,128]{1,0:T(8,128)S(1)}, u32[]{:S(2)}, u32[]{:S(2)}) collective-permute-start(f32[256,128]{1,0:T(8,128)S(1)} %pad_maximum_fusion.1), channel_id=1, source_target_pairs={{0,32},{32,0},{64,96},{96,64},{1,33},{33,1},{65,97},{97,65},{2,34}... | collective-permute-start | bytes 393224 | tf_op jit(solution)/shard_map/ppermute | solution.py:482
  74.8 7.1 %collective-permute-start.22 = (f32[1024,128]{1,0:T(8,128)S(1)}, f32[1024,128]{1,0:T(8,128)S(1)}, u32[]{:S(2)}, u32[]{:S(2)}) collective-permute-start(f32[1024,128]{1,0:T(8,128)S(1)} %constant_dynamic-update-slice_fusion.15.near), channel_id=1, source_target_pairs={{0,16},{16,0},{1,17},{17,1},{2,18},{18,2},{3,19},{19,3},{4,20},{20... | collective-permute-start | bytes 1572872 | tf_op jit(solution)/shard_map/ppermute | solution.py:482
  88.5 4.7 %collective-permute-start.24 = (f32[136,128]{1,0:T(8,128)S(1)}, f32[136,128]{1,0:T(8,128)S(1)}, u32[]{:S(2)}, u32[]{:S(2)}) collective-permute-start(f32[136,128]{1,0:T(8,128)S(1)} %get-tuple-element.77), channel_id=1, source_target_pairs={{0,2},{1,3},{2,0},{3,1},{4,6},{5,7},{6,4},{7,5},{8,10},{9,11},{10,... | collective-permute-start | bytes 208904 | tf_op jit(solution)/shard_map/ppermute | solution.py:482
  94.3 4.6 %collective-permute-start.27 = (f32[128,128]{1,0:T(8,128)S(1)}, f32[128,128]{1,0:T(8,128)S(1)}, u32[]{:S(2)}, u32[]{:S(2)}) collective-permute-start(f32[128,128]{1,0:T(8,128)S(1)} %step.2.foot), channel_id=1, source_target_pairs={{0,2},{1,3},{2,0},{3,1},{4,6},{5,7},{6,4},{7,5},{8,10},{9,11},{10,... | collective-permute-start | bytes 196616 | tf_op jit(solution)/shard_map/ppermute | solution.py:482
  101.6 5.2 %collective-permute-start.29 = (f32[4,264,128]{2,1,0:T(8,128)S(1)}, f32[4,264,128]{2,1,0:T(8,128)S(1)}, u32[]{:S(2)}, u32[]{:S(2)}) collective-permute-start(f32[4,264,128]{2,1,0:T(8,128)S(1)} %get-tuple-element.89), channel_id=1, source_target_pairs={{0,16},{16,0},{1,17},{17,1},{2,18},{18,2},{3,19},{19,3},{4,20},{20... | collective-permute-start | bytes 1622024 | tf_op jit(solution)/shard_map/ppermute | solution.py:482
  106.9 6.4 %collective-permute-start.30 = (f32[264,128]{1,0:T(8,128)S(1)}, f32[264,128]{1,0:T(8,128)S(1)}, u32[]{:S(2)}, u32[]{:S(2)}) collective-permute-start(f32[264,128]{1,0:T(8,128)S(1)} %get-tuple-element.91), channel_id=1, source_target_pairs={{0,64},{32,96},{64,0},{96,32},{1,65},{33,97},{65,1},{97,33},{2,66}... | collective-permute-start | bytes 405512 | tf_op jit(solution)/shard_map/ppermute | solution.py:482
  107.4 7.3 %collective-permute-start.31 = (f32[264,128]{1,0:T(8,128)S(1)}, f32[264,128]{1,0:T(8,128)S(1)}, u32[]{:S(2)}, u32[]{:S(2)}) collective-permute-start(f32[264,128]{1,0:T(8,128)S(1)} %get-tuple-element.92), channel_id=1, source_target_pairs={{0,32},{32,0},{64,96},{96,64},{1,33},{33,1},{65,97},{97,65},{2,34}... | collective-permute-start | bytes 405512 | tf_op jit(solution)/shard_map/ppermute | solution.py:482
  108.5 8.2 %collective-permute-start.32 = (f32[264,128]{1,0:T(8,128)S(1)}, f32[264,128]{1,0:T(8,128)S(1)}, u32[]{:S(2)}, u32[]{:S(2)}) collective-permute-start(f32[264,128]{1,0:T(8,128)S(1)} %get-tuple-element.93), channel_id=1, source_target_pairs={{0,96},{32,64},{64,32},{96,0},{1,97},{33,65},{65,33},{97,1},{2,98}... | collective-permute-start | bytes 405512 | tf_op jit(solution)/shard_map/ppermute | solution.py:482
  116.7 4.7 %collective-permute-start.33 = (f32[72,128]{1,0:T(8,128)S(1)}, f32[72,128]{1,0:T(8,128)S(1)}, u32[]{:S(2)}, u32[]{:S(2)}) collective-permute-start(f32[72,128]{1,0:T(8,128)S(1)} %get-tuple-element.95), channel_id=1, source_target_pairs={{0,12},{4,8},{8,4},{12,0},{1,13},{5,9},{9,5},{13,1},{2,14},{6,10},... | collective-permute-start | bytes 110600 | tf_op jit(solution)/shard_map/ppermute | solution.py:482
  123.0 5.7 %collective-permute-start.36 = (f32[72,128]{1,0:T(8,128)S(1)}, f32[72,128]{1,0:T(8,128)S(1)}, u32[]{:S(2)}, u32[]{:S(2)}) collective-permute-start(f32[72,128]{1,0:T(8,128)S(1)} %fold_z.3.own), channel_id=1, source_target_pairs={{0,140},{4,136},{8,132},{12,128},{128,12},{132,8},{136,4},{140,0},... | collective-permute-start | bytes 110600 | tf_op jit(solution)/shard_map/ppermute | solution.py:482
  128.8 4.7 %collective-permute-start.39 = (f32[64,128]{1,0:T(8,128)S(1)}, f32[64,128]{1,0:T(8,128)S(1)}, u32[]{:S(2)}, u32[]{:S(2)}) collective-permute-start(f32[64,128]{1,0:T(8,128)S(1)} %update.3), channel_id=1, source_target_pairs={{0,12},{4,8},{8,4},{12,0},{1,13},{5,9},{9,5},{13,1},{2,14},{6,10},... | collective-permute-start | bytes 98312 | tf_op jit(solution)/shard_map/ppermute | solution.py:482
  134.5 7.1 %collective-permute-start.42 = (f32[256,128]{1,0:T(8,128)S(1)}, f32[256,128]{1,0:T(8,128)S(1)}, u32[]{:S(2)}, u32[]{:S(2)}) collective-permute-start(f32[256,128]{1,0:T(8,128)S(1)} %pad_maximum_fusion.2), channel_id=1, source_target_pairs={{0,96},{32,64},{64,32},{96,0},{1,97},{33,65},{65,33},{97,1},{2,98}... | collective-permute-start | bytes 393224 | tf_op jit(solution)/shard_map/ppermute | solution.py:482
  134.9 6.8 %collective-permute-start.41 = (f32[256,128]{1,0:T(8,128)S(1)}, f32[256,128]{1,0:T(8,128)S(1)}, u32[]{:S(2)}, u32[]{:S(2)}) collective-permute-start(f32[256,128]{1,0:T(8,128)S(1)} %pad_maximum_fusion.2), channel_id=1, source_target_pairs={{0,64},{32,96},{64,0},{96,32},{1,65},{33,97},{65,1},{97,33},{2,66}... | collective-permute-start | bytes 393224 | tf_op jit(solution)/shard_map/ppermute | solution.py:482
  136.8 4.9 %collective-permute-start.40 = (f32[256,128]{1,0:T(8,128)S(1)}, f32[256,128]{1,0:T(8,128)S(1)}, u32[]{:S(2)}, u32[]{:S(2)}) collective-permute-start(f32[256,128]{1,0:T(8,128)S(1)} %pad_maximum_fusion.2), channel_id=1, source_target_pairs={{0,32},{32,0},{64,96},{96,64},{1,33},{33,1},{65,97},{97,65},{2,34}... | collective-permute-start | bytes 393224 | tf_op jit(solution)/shard_map/ppermute | solution.py:482
  141.7 7.0 %collective-permute-start.43 = (f32[1024,128]{1,0:T(8,128)S(1)}, f32[1024,128]{1,0:T(8,128)S(1)}, u32[]{:S(2)}, u32[]{:S(2)}) collective-permute-start(f32[1024,128]{1,0:T(8,128)S(1)} %constant_dynamic-update-slice_fusion.22.near), channel_id=1, source_target_pairs={{0,16},{16,0},{1,17},{17,1},{2,18},{18,2},{3,19},{19,3},{4,20},{20... | collective-permute-start | bytes 1572872 | tf_op jit(solution)/shard_map/ppermute | solution.py:482
  154.1 4.7 %collective-permute-start.45 = (f32[136,128]{1,0:T(8,128)S(1)}, f32[136,128]{1,0:T(8,128)S(1)}, u32[]{:S(2)}, u32[]{:S(2)}) collective-permute-start(f32[136,128]{1,0:T(8,128)S(1)} %get-tuple-element.99), channel_id=1, source_target_pairs={{0,2},{1,3},{2,0},{3,1},{4,6},{5,7},{6,4},{7,5},{8,10},{9,11},{10,... | collective-permute-start | bytes 208904 | tf_op jit(solution)/shard_map/ppermute | solution.py:482
  (18 other events, 71.2 us)
where the time goes:
time: 167 us; the launch traced here: 166 us
  starting transfers between devices  83 us (50%)
  waiting for transfers between devices  54.2 us (32%)
  Pallas kernels  24.9 us (15%)
  local copies, waits for them, and re-layouts  2.38 us (1%)
    ppermute x50, starting transfers between devices, swapped(): return lax.ppermute(x, axis, [(i, i ^ bits) for i in range(n)])  83 us
    ppermute x50, waiting for transfers between devices, swapped(): return lax.ppermute(x, axis, [(i, i ^ bits) for i in range(n)])  54.2 us
    pallas_call x6, Pallas kernels, gradient(): pl.pallas_call(functools.partial(grad_kernel, k), in_specs=[VM] * 3, out_...  5.22 us
    pallas_call x1, Pallas kernels, first(): pl.pallas_call(first_kernel, in_specs=[VM, HB, HB], out_specs=[VM] * 7, o...  3.74 us
    pallas_call x2, Pallas kernels, picked_gradient(): pl.pallas_call(functools.partial(picked_grad_kernel, k), in_specs=[VM] *...  3.34 us
  transfers between devices with their start and end apart: 50, of which 34 were waited for; matrix products, arithmetic and copies ran while one was open for 1% of the time, Pallas kernels for 8%

commit v1 on v0

--- a/solution.py
+++ b/solution.py
@@ -17,7 +17,6 @@
 BLOCKS = ("zh", "y", "c", "zl")
 NGROUP = 4
 GT = 16
-UNROLL = 8
 HALF = 1024
 NBLK = 16
 ROWS = 72
@@ -114,8 +113,9 @@
         comp = entry[x ^ k]
         owner = comp >> 5
         ozh, oy, oc, ozl = owner >> 5, (owner >> 3) & 3, (owner >> 2) & 1, owner & 3
-        block = ((oc ^ c) * 4 + (oy ^ y)) * 4 + (ozl ^ (3 * ozh) ^ zl ^ (3 * zh))
-        index = jnp.where(comp < K, block * 64 + (ozh ^ zh) * 32 + (comp & 31), K)
+        row = ((oc ^ c) * 4 + (oy ^ y)) * 256 + (comp & 31)
+        index = row + (ozl ^ (3 * ozh) ^ zl ^ (3 * zh)) * 64 + (ozh ^ zh) * 32
+        index = jnp.where(comp < K, index, K)
         place[:, s] = index
         at = as_column(index.astype(f32), 128)
         column[s, :] = at.astype(jnp.int32)
@@ -171,7 +171,7 @@
     )
 
 
-def scatter(half, place, both, curv, out):
+def scatter(half, place, both, curv, out, looped):
     n = place.shape[1]
     lane = lax.broadcasted_iota(jnp.int32, (256, n), 0)
     inside = jnp.where(lane[:128] == place % 64, 1.0, 0.0).astype(bf16)
@@ -182,32 +182,39 @@
     for k in range(4):
         out[k, 256:, :] = dens[k * 4 : k * 4 + 8]
 
-    def block_rows(k, carry):
+    def rows(k, carry):
         hot = jnp.where(lane + (half * HALF + k * 256) == place, 1.0, 0.0).astype(bf16)
-        got = nn(hot, both)
+        got = nn(hot, both[...])
         out[k, :256, :] = got[:, :128] + got[:, 128:]
         return carry
 
-    lax.fori_loop(0, 4, block_rows, 0)
-
-
-def picked_from(half, column, part, add, out):
-    both = jnp.concatenate(split(part[...]), axis=1)
-    lane = lax.broadcasted_iota(jnp.int32, (256, HALF), 1) + half * HALF
+    if looped:
+        lax.fori_loop(0, 4, rows, 0)
+    else:
+        for k in range(4):
+            rows(k, 0)
+
+
+def picked_from_far(column, far, near, out):
+    both = jnp.concatenate(split(far[...]), axis=1)
+    at = column[...]
+    lane = lax.broadcasted_iota(jnp.int32, (at.shape[0], HALF), 1) + HALF
+    got = nn(jnp.where(lane == at, 1.0, 0.0).astype(bf16), both)
+    out[...] = got[:, :128] + got[:, 128:] + near[...]
+
+
+def near_kernel(column, near, out):
+    both = jnp.concatenate(split(near[...]), axis=1)
+    lane = lax.broadcasted_iota(jnp.int32, (256, HALF), 1)
 
     def some(i, carry):
         s = pl.ds(pl.multiple_of(i * 256, 256), 256)
         hot = jnp.where(lane == column[s, :], 1.0, 0.0).astype(bf16)
         got = nn(hot, both)
-        got = got[:, :128] + got[:, 128:]
-        out[s, :] = got if add is None else got + add[s, :]
+        out[s, :] = got[:, :128] + got[:, 128:]
         return carry
 
     lax.fori_loop(0, 2, some, 0)
-
-
-def near_kernel(column, near, out):
-    picked_from(0, column, near, None, out)
 
 
 def pick_near(column, near):
@@ -231,11 +238,11 @@
     row = jnp.concatenate(rows, axis=1)
     both[...] = two
     curv[...] = jnp.broadcast_to(row, (8, 512))
-    scatter(1, place[...], two, row, other)
+    scatter(1, place[...], two, row, other, False)
 
 
 def numer_kernel(place, column, proj, gram, got, far, other, both, curv, work):
-    picked_from(1, column, far, got, work)
+    picked_from_far(column, far, got, work)
     rows = []
     for g in range(NGROUP):
         s = slice(g * 128, (g + 1) * 128)
@@ -257,7 +264,7 @@
 
 
 def mine_kernel(place, both, curv, mine):
-    scatter(0, place[...], both[...], curv[:1, :], mine)
+    scatter(0, place[...], both, curv[:1, :], mine, True)
 
 
 def scatter_mine(place, both, curv):
@@ -351,21 +358,15 @@
     p = picked[k * 128 : (k + 1) * 128, :]
     gram = jnp.where(same_tile(), nt3(p, p), 0.0)
     out[128:, :] = jnp.broadcast_to(jnp.sum(gram, axis=0, keepdims=True), (8, 128))
-    out[:128, :] = -nn3(gram, foot[k * 128 : (k + 1) * 128, :])
-
-    def tiles(i, carry):
-        for j in range(UNROLL):
-            t = i * UNROLL + j
-            at = pl.ds(pl.multiple_of(k * 128 + t * SLOTS, SLOTS), SLOTS)
-            rows = pl.ds(pl.multiple_of(t * SLOTS, SLOTS), SLOTS)
-            out[rows, :] += correlate(picked[at, :], pairs[k * GT + t])
-        return carry
-
-    lax.fori_loop(0, GT // UNROLL, tiles, 0)
+    parts = []
+    for t in range(GT):
+        parts.append(correlate(p[t * SLOTS : (t + 1) * SLOTS], pairs[k * GT + t]))
+    less = nn3(gram, foot[k * 128 : (k + 1) * 128, :])
+    out[:128, :] = jnp.concatenate(parts, axis=0) - less
 
 
 def picked_grad_kernel(k, column, got, far, foot, pairs, picked, out):
-    picked_from(1, column, far, got, picked)
+    picked_from_far(column, far, got, picked)
     grad_piece(k, picked, foot, pairs, out)
 
 
@@ -418,16 +419,11 @@
     f = foot[...]
     gram = jnp.where(same_tile(), nt3(f, f), 0.0)
     curv[...] = jnp.broadcast_to(jnp.sum(gram, axis=0, keepdims=True), (8, 128))
-    work[...] = -nn3(gram, picked[k * 128 : (k + 1) * 128, :])
-
-    def tiles(i, carry):
-        for j in range(UNROLL):
-            t = i * UNROLL + j
-            rows = pl.ds(pl.multiple_of(t * SLOTS, SLOTS), SLOTS)
-            work[rows, :] += project(foot[rows, :], pairs[k * GT + t])
-        return carry
-
-    lax.fori_loop(0, GT // UNROLL, tiles, 0)
+    parts = []
+    for t in range(GT):
+        parts.append(project(f[t * SLOTS : (t + 1) * SLOTS], pairs[k * GT + t]))
+    less = nn3(gram, picked[k * 128 : (k + 1) * 128, :])
+    work[...] = jnp.concatenate(parts, axis=0) - less
 
 
 def projected(k, foot, picked, pairs):
@@ -489,7 +485,7 @@
 def summed_blocks(place, other, both, curv):
     came = swapped(other, "c", 1)
     ys = fold_core(scatter_mine(place, both, curv), came)
-    zs = fold_y([ys[0]] + [swapped(ys[k], "y", k) for k in (2, 1, 3)])
+    zs = fold_y([ys[0]] + [swapped(ys[k], "y", k) for k in (3, 2, 1)])
     own = fold_z([zs[0]] + [swapped(zs[k], "zl", k) for k in (3, 2, 1)])
     return own, across(own)
 
@@ -511,11 +507,15 @@
 
 
 def local(movie, traces, entry_comp, footprints):
-    own = jnp.concatenate([traces, across(traces)], axis=0)
     entry = entry_comp.reshape(NGROUP, 1, 128)
-    near = gathered(gathered(own, "zl"), "y")
+    twin, entry = lax.optimization_barrier((across(traces), entry))
+    own = jnp.concatenate([traces, twin], axis=0)
+    part = gathered(own, "zl")
     made = first(entry, movie, footprints.reshape(-1, TILE))
-    near, place, column, valid, foot, pairs, proj, gram = lax.optimization_barrier((near, *made))
+    part, place, column, valid, foot, pairs, proj, gram = lax.optimization_barrier(
+        (part, *made)
+    )
+    near = gathered(part, "y")
     far = swapped(near, "c", 1)
     sums = numerators(place, column, proj, gram, pick_near(column, near), far)
     for step in range(ITERS):

time: 167 us -> 159 us (0.952)
  Pallas kernels: 24.9 us -> 19.4 us
  waiting for transfers between devices: 54.2 us -> 49.5 us
  starting transfers between devices: 83 us -> 85.1 us
    ppermute x50, waiting for transfers between devices: 54.2 us -> 49.5 us  [swapped(): return lax.ppermute(x, axis, [(i, i ^ bits) for i in range(n)])]
    pallas_call x6, Pallas kernels: 5.22 us -> 2.98 us  [gradient(): pl.pallas_call(functools.partial(grad_kernel, k), in_specs=[VM] * 3, out_...]
    ppermute x50, starting transfers between devices: 83 us -> 85.1 us  [swapped(): return lax.ppermute(x, axis, [(i, i ^ bits) for i in range(n)])]
  transfers between devices with their start and end apart: 50 -> 50, of which waited for: 34 -> 33; matrix products, arithmetic and copies ran while one was open for 1% -> 1% of each run, Pallas kernels for 8% -> 7%
where the time goes in v1:
time: 159 us; the launch traced here: 158 us
  starting transfers between devices  85.1 us (54%)
  waiting for transfers between devices  49.5 us (31%)
  Pallas kernels  19.4 us (12%)
  local copies, waits for them, and re-layouts  2.38 us (1%)
    ppermute x50, starting transfers between devices, swapped(): return lax.ppermute(x, axis, [(i, i ^ bits) for i in range(n)])  85.1 us
    ppermute x50, waiting for transfers between devices, swapped(): return lax.ppermute(x, axis, [(i, i ^ bits) for i in range(n)])  49.5 us
    pallas_call x1, Pallas kernels, first(): pl.pallas_call(first_kernel, in_specs=[VM, HB, HB], out_specs=[VM] * 7, o...  3.73 us
  transfers between devices with their start and end apart: 50, of which 33 were waited for; matrix products, arithmetic and copies ran while one was open for 1% of the time, Pallas kernels for 7%

profile of v1, /device:TPU:1, one launch (start us, length us, event | category | flops | bytes accessed | tf_op | source)
XLA Modules:
  0.0 157.5 jit_solution(18117372051040304621)
XLA Ops:
  0.6 6.5 %collective-permute-start = (f32[32,128]{1,0:T(8,128)}, f32[32,128]{1,0:T(8,128)S(1)}, u32[]{:S(2)}, u32[]{:S(2)}) collective-permute-start(f32[32,128]{1,0:T(8,128)} %param.5), channel_id=1, source_target_pairs={{0,140},{4,136},{8,132},{12,128},{128,12},{132,8},{136,4},{140,0},... | collective-permute-start | bytes 49160 | tf_op jit(solution)/shard_map/ppermute | solution.py:478
  8.7 1.7 %collective-permute-start.1 = (f32[64,128]{1,0:T(8,128)S(1)}, f32[64,128]{1,0:T(8,128)S(1)}, u32[]{:S(2)}, u32[]{:S(2)}) collective-permute-start(f32[64,128]{1,0:T(8,128)S(1)} %get-tuple-element.104.traces), channel_id=1, source_target_pairs={{0,4},{4,0},{8,12},{12,8},{1,5},{5,1},{9,13},{13,9},{2,6},{6,2},{1... | collective-permute-start | bytes 98312 | tf_op jit(solution)/shard_map/ppermute | solution.py:478
  10.5 1.6 %collective-permute-start.3 = (f32[64,128]{1,0:T(8,128)S(1)}, f32[64,128]{1,0:T(8,128)S(1)}, u32[]{:S(2)}, u32[]{:S(2)}) collective-permute-start(f32[64,128]{1,0:T(8,128)S(1)} %get-tuple-element.104.traces), channel_id=1, source_target_pairs={{0,12},{4,8},{8,4},{12,0},{1,13},{5,9},{9,5},{13,1},{2,14},{6,10},... | collective-permute-start | bytes 98312 | tf_op jit(solution)/shard_map/ppermute | solution.py:478
  12.1 3.7 %first.1 = (s32[1,512]{1,0:T(1,128)S(1)}, s32[512,1]{1,0:T(8,128)S(1)}, f32[512,1]{1,0:T(8,128)S(1)}, f32[512,128]{1,0:T(8,128)S(1)}, bf16[64,256,128]{2,1,0:T(8...) custom-call(s32[4,1,128]{2,1,0:T(1,128)S(1)} %bitcast.3, f32[8192,128]{1,0:T(8,128)} %movie.1, ...), custom_call_target="tpu_custom_call" | custom-call | flops 67108864 | bytes 1048576 | tf_op jit(solution)/shard_map/first/pallas_call | solution.py:146
  17.5 1.9 %collective-permute-start.6 = (f32[256,128]{1,0:T(8,128)S(1)}, f32[256,128]{1,0:T(8,128)S(1)}, u32[]{:S(2)}, u32[]{:S(2)}) collective-permute-start(f32[256,128]{1,0:T(8,128)S(1)} %constant_dynamic-update-slice_fusion.2), channel_id=1, source_target_pairs={{0,96},{32,64},{64,32},{96,0},{1,97},{33,65},{65,33},{97,1},{2,98}... | collective-permute-start | bytes 393224 | tf_op jit(solution)/shard_map/ppermute | solution.py:478
  20.1 5.1 %collective-permute-done.5 = f32[256,128]{1,0:T(8,128)S(1)} collective-permute-done((f32[256,128]{1,0:T(8,128)S(1)}, f32[256,128]{1,0:T(8,128)S(1)}, u32[]{:S(2)}, u32[]{:S(2)}) %collective-permute-start.5) | collective-permute-done | bytes 131104 | tf_op jit(solution)/shard_map/ppermute | solution.py:478
  25.2 3.9 %collective-permute-start.7 = (f32[1024,128]{1,0:T(8,128)S(1)}, f32[1024,128]{1,0:T(8,128)S(1)}, u32[]{:S(2)}, u32[]{:S(2)}) collective-permute-start(f32[1024,128]{1,0:T(8,128)S(1)} %constant_dynamic-update-slice_fusion.7.near), channel_id=1, source_target_pairs={{0,16},{16,0},{1,17},{17,1},{2,18},{18,2},{3,19},{19,3},{4,20},{20... | collective-permute-start | bytes 1572872 | tf_op jit(solution)/shard_map/ppermute | solution.py:478
  30.7 1.5 numerators.1
  37.6 5.3 %collective-permute-done.9.b = f32[264,128]{1,0:T(8,128)S(1)} collective-permute-done((f32[264,128]{1,0:T(8,128)S(1)}, f32[264,128]{1,0:T(8,128)S(1)}, u32[]{:S(2)}, u32[]{:S(2)}) %collective-permute-start.9) | collective-permute-done | bytes 135200 | tf_op jit(solution)/shard_map/ppermute | solution.py:478
  43.7 1.6 %collective-permute-start.12 = (f32[72,128]{1,0:T(8,128)S(1)}, f32[72,128]{1,0:T(8,128)S(1)}, u32[]{:S(2)}, u32[]{:S(2)}) collective-permute-start(f32[72,128]{1,0:T(8,128)S(1)} %get-tuple-element.75), channel_id=1, source_target_pairs={{0,12},{4,8},{8,4},{12,0},{1,13},{5,9},{9,5},{13,1},{2,14},{6,10},... | collective-permute-start | bytes 110600 | tf_op jit(solution)/shard_map/ppermute | solution.py:478
  49.6 4.1 %collective-permute-start.15 = (f32[72,128]{1,0:T(8,128)S(1)}, f32[72,128]{1,0:T(8,128)S(1)}, u32[]{:S(2)}, u32[]{:S(2)}) collective-permute-start(f32[72,128]{1,0:T(8,128)S(1)} %fold_z.2.own), channel_id=1, source_target_pairs={{0,140},{4,136},{8,132},{12,128},{128,12},{132,8},{136,4},{140,0},... | collective-permute-start | bytes 110600 | tf_op jit(solution)/shard_map/ppermute | solution.py:478
  55.2 1.6 %collective-permute-start.18 = (f32[64,128]{1,0:T(8,128)S(1)}, f32[64,128]{1,0:T(8,128)S(1)}, u32[]{:S(2)}, u32[]{:S(2)}) collective-permute-start(f32[64,128]{1,0:T(8,128)S(1)} %update.2.traces), channel_id=1, source_target_pairs={{0,12},{4,8},{8,4},{12,0},{1,13},{5,9},{9,5},{13,1},{2,14},{6,10},... | collective-permute-start | bytes 98312 | tf_op jit(solution)/shard_map/ppermute | solution.py:478
  56.8 1.4 collective-permute-start.17
  64.4 3.7 %collective-permute-done.19 = f32[256,128]{1,0:T(8,128)S(1)} collective-permute-done((f32[256,128]{1,0:T(8,128)S(1)}, f32[256,128]{1,0:T(8,128)S(1)}, u32[]{:S(2)}, u32[]{:S(2)}) %collective-permute-start.19) | collective-permute-done | bytes 131104 | tf_op jit(solution)/shard_map/ppermute | solution.py:478
  68.2 6.8 %collective-permute-start.22 = (f32[1024,128]{1,0:T(8,128)S(1)}, f32[1024,128]{1,0:T(8,128)S(1)}, u32[]{:S(2)}, u32[]{:S(2)}) collective-permute-start(f32[1024,128]{1,0:T(8,128)S(1)} %constant_dynamic-update-slice_fusion.11.near), channel_id=1, source_target_pairs={{0,16},{16,0},{1,17},{17,1},{2,18},{18,2},{3,19},{19,3},{4,20},{20... | collective-permute-start | bytes 1572872 | tf_op jit(solution)/shard_map/ppermute | solution.py:478
  76.6 1.4 picked_gradient.2
  80.2 1.9 %collective-permute-start.25 = (f32[136,128]{1,0:T(8,128)S(1)}, f32[136,128]{1,0:T(8,128)S(1)}, u32[]{:S(2)}, u32[]{:S(2)}) collective-permute-start(f32[136,128]{1,0:T(8,128)S(1)} %gradient.8), channel_id=1, source_target_pairs={{0,3},{1,2},{2,1},{3,0},{4,7},{5,6},{6,5},{7,4},{8,11},{9,10},{10,... | collective-permute-start | bytes 208904 | tf_op jit(solution)/shard_map/ppermute | solution.py:478
  84.6 2.2 %collective-permute-done.24.c = f32[136,128]{1,0:T(8,128)S(1)} collective-permute-done((f32[136,128]{1,0:T(8,128)S(1)}, f32[136,128]{1,0:T(8,128)S(1)}, u32[]{:S(2)}, u32[]{:S(2)}) %collective-permute-start.24) | collective-permute-done | bytes 69664 | tf_op jit(solution)/shard_map/ppermute | solution.py:478
  93.8 3.6 %collective-permute-start.29 = (f32[4,264,128]{2,1,0:T(8,128)S(1)}, f32[4,264,128]{2,1,0:T(8,128)S(1)}, u32[]{:S(2)}, u32[]{:S(2)}) collective-permute-start(f32[4,264,128]{2,1,0:T(8,128)S(1)} %get-tuple-element.93), channel_id=1, source_target_pairs={{0,16},{16,0},{1,17},{17,1},{2,18},{18,2},{3,19},{19,3},{4,20},{20... | collective-permute-start | bytes 1622024 | tf_op jit(solution)/shard_map/ppermute | solution.py:478
  102.4 5.3 %collective-permute-done.30.b = f32[264,128]{1,0:T(8,128)S(1)} collective-permute-done((f32[264,128]{1,0:T(8,128)S(1)}, f32[264,128]{1,0:T(8,128)S(1)}, u32[]{:S(2)}, u32[]{:S(2)}) %collective-permute-start.30) | collective-permute-done | bytes 135200 | tf_op jit(solution)/shard_map/ppermute | solution.py:478
  108.5 1.6 %collective-permute-start.33 = (f32[72,128]{1,0:T(8,128)S(1)}, f32[72,128]{1,0:T(8,128)S(1)}, u32[]{:S(2)}, u32[]{:S(2)}) collective-permute-start(f32[72,128]{1,0:T(8,128)S(1)} %get-tuple-element.99), channel_id=1, source_target_pairs={{0,12},{4,8},{8,4},{12,0},{1,13},{5,9},{9,5},{13,1},{2,14},{6,10},... | collective-permute-start | bytes 110600 | tf_op jit(solution)/shard_map/ppermute | solution.py:478
  110.2 1.9 %collective-permute-start.35 = (f32[72,128]{1,0:T(8,128)S(1)}, f32[72,128]{1,0:T(8,128)S(1)}, u32[]{:S(2)}, u32[]{:S(2)}) collective-permute-start(f32[72,128]{1,0:T(8,128)S(1)} %get-tuple-element.101), channel_id=1, source_target_pairs={{0,4},{4,0},{8,12},{12,8},{1,5},{5,1},{9,13},{13,9},{2,6},{6,2},{1... | collective-permute-start | bytes 110600 | tf_op jit(solution)/shard_map/ppermute | solution.py:478
  114.4 3.8 %collective-permute-start.36 = (f32[72,128]{1,0:T(8,128)S(1)}, f32[72,128]{1,0:T(8,128)S(1)}, u32[]{:S(2)}, u32[]{:S(2)}) collective-permute-start(f32[72,128]{1,0:T(8,128)S(1)} %fold_z.3.own), channel_id=1, source_target_pairs={{0,140},{4,136},{8,132},{12,128},{128,12},{132,8},{136,4},{140,0},... | collective-permute-start | bytes 110600 | tf_op jit(solution)/shard_map/ppermute | solution.py:478
  119.6 2.0 %collective-permute-start.39 = (f32[64,128]{1,0:T(8,128)S(1)}, f32[64,128]{1,0:T(8,128)S(1)}, u32[]{:S(2)}, u32[]{:S(2)}) collective-permute-start(f32[64,128]{1,0:T(8,128)S(1)} %update.3), channel_id=1, source_target_pairs={{0,12},{4,8},{8,4},{12,0},{1,13},{5,9},{9,5},{13,1},{2,14},{6,10},... | collective-permute-start | bytes 98312 | tf_op jit(solution)/shard_map/ppermute | solution.py:478
  126.8 1.4 collective-permute-start.41
  129.1 3.7 %collective-permute-done.40 = f32[256,128]{1,0:T(8,128)S(1)} collective-permute-done((f32[256,128]{1,0:T(8,128)S(1)}, f32[256,128]{1,0:T(8,128)S(1)}, u32[]{:S(2)}, u32[]{:S(2)}) %collective-permute-start.40) | collective-permute-done | bytes 131104 | tf_op jit(solution)/shard_map/ppermute | solution.py:478
  132.9 6.9 %collective-permute-start.43 = (f32[1024,128]{1,0:T(8,128)S(1)}, f32[1024,128]{1,0:T(8,128)S(1)}, u32[]{:S(2)}, u32[]{:S(2)}) collective-permute-start(f32[1024,128]{1,0:T(8,128)S(1)} %constant_dynamic-update-slice_fusion.18.near), channel_id=1, source_target_pairs={{0,16},{16,0},{1,17},{17,1},{2,18},{18,2},{3,19},{19,3},{4,20},{20... | collective-permute-start | bytes 1572872 | tf_op jit(solution)/shard_map/ppermute | solution.py:478
  141.3 1.4 picked_gradient.3
  147.6 1.4 collective-permute-done.46.d
  149.0 1.5 collective-permute-done.45.c
  150.6 1.5 collective-permute-start.49
  155.1 1.8 %collective-permute-done.48.f2 = f32[128,128]{1,0:T(8,128)S(1)} collective-permute-done((f32[128,128]{1,0:T(8,128)S(1)}, f32[128,128]{1,0:T(8,128)S(1)}, u32[]{:S(2)}, u32[]{:S(2)}) %collective-permute-start.48) | collective-permute-done | bytes 65568 | tf_op jit(solution)/shard_map/ppermute | solution.py:478
  (128 shorter events, 62.5 us)
Async XLA Ops:
  0.6 8.1 %collective-permute-start = (f32[32,128]{1,0:T(8,128)}, f32[32,128]{1,0:T(8,128)S(1)}, u32[]{:S(2)}, u32[]{:S(2)}) collective-permute-start(f32[32,128]{1,0:T(8,128)} %param.5), channel_id=1, source_target_pairs={{0,140},{4,136},{8,132},{12,128},{128,12},{132,8},{136,4},{140,0},... | collective-permute-start | bytes 49160 | tf_op jit(solution)/shard_map/ppermute | solution.py:478
  8.7 7.1 %collective-permute-start.1 = (f32[64,128]{1,0:T(8,128)S(1)}, f32[64,128]{1,0:T(8,128)S(1)}, u32[]{:S(2)}, u32[]{:S(2)}) collective-permute-start(f32[64,128]{1,0:T(8,128)S(1)} %get-tuple-element.104.traces), channel_id=1, source_target_pairs={{0,4},{4,0},{8,12},{12,8},{1,5},{5,1},{9,13},{13,9},{2,6},{6,2},{1... | collective-permute-start | bytes 98312 | tf_op jit(solution)/shard_map/ppermute | solution.py:478
  10.5 5.6 %collective-permute-start.3 = (f32[64,128]{1,0:T(8,128)S(1)}, f32[64,128]{1,0:T(8,128)S(1)}, u32[]{:S(2)}, u32[]{:S(2)}) collective-permute-start(f32[64,128]{1,0:T(8,128)S(1)} %get-tuple-element.104.traces), channel_id=1, source_target_pairs={{0,12},{4,8},{8,4},{12,0},{1,13},{5,9},{9,5},{13,1},{2,14},{6,10},... | collective-permute-start | bytes 98312 | tf_op jit(solution)/shard_map/ppermute | solution.py:478
  17.5 7.8 %collective-permute-start.6 = (f32[256,128]{1,0:T(8,128)S(1)}, f32[256,128]{1,0:T(8,128)S(1)}, u32[]{:S(2)}, u32[]{:S(2)}) collective-permute-start(f32[256,128]{1,0:T(8,128)S(1)} %constant_dynamic-update-slice_fusion.2), channel_id=1, source_target_pairs={{0,96},{32,64},{64,32},{96,0},{1,97},{33,65},{65,33},{97,1},{2,98}... | collective-permute-start | bytes 393224 | tf_op jit(solution)/shard_map/ppermute | solution.py:478
  19.4 5.8 %collective-permute-start.5 = (f32[256,128]{1,0:T(8,128)S(1)}, f32[256,128]{1,0:T(8,128)S(1)}, u32[]{:S(2)}, u32[]{:S(2)}) collective-permute-start(f32[256,128]{1,0:T(8,128)S(1)} %constant_dynamic-update-slice_fusion.2), channel_id=1, source_target_pairs={{0,64},{32,96},{64,0},{96,32},{1,65},{33,97},{65,1},{97,33},{2,66}... | collective-permute-start | bytes 393224 | tf_op jit(solution)/shard_map/ppermute | solution.py:478
  25.2 5.5 %collective-permute-start.7 = (f32[1024,128]{1,0:T(8,128)S(1)}, f32[1024,128]{1,0:T(8,128)S(1)}, u32[]{:S(2)}, u32[]{:S(2)}) collective-permute-start(f32[1024,128]{1,0:T(8,128)S(1)} %constant_dynamic-update-slice_fusion.7.near), channel_id=1, source_target_pairs={{0,16},{16,0},{1,17},{17,1},{2,18},{18,2},{3,19},{19,3},{4,20},{20... | collective-permute-start | bytes 1572872 | tf_op jit(solution)/shard_map/ppermute | solution.py:478
  34.3 8.6 %collective-permute-start.9 = (f32[264,128]{1,0:T(8,128)S(1)}, f32[264,128]{1,0:T(8,128)S(1)}, u32[]{:S(2)}, u32[]{:S(2)}) collective-permute-start(f32[264,128]{1,0:T(8,128)S(1)} %get-tuple-element.71), channel_id=1, source_target_pairs={{0,96},{32,64},{64,32},{96,0},{1,97},{33,65},{65,33},{97,1},{2,98}... | collective-permute-start | bytes 405512 | tf_op jit(solution)/shard_map/ppermute | solution.py:478
  35.4 7.5 %collective-permute-start.10 = (f32[264,128]{1,0:T(8,128)S(1)}, f32[264,128]{1,0:T(8,128)S(1)}, u32[]{:S(2)}, u32[]{:S(2)}) collective-permute-start(f32[264,128]{1,0:T(8,128)S(1)} %get-tuple-element.72), channel_id=1, source_target_pairs={{0,64},{32,96},{64,0},{96,32},{1,65},{33,97},{65,1},{97,33},{2,66}... | collective-permute-start | bytes 405512 | tf_op jit(solution)/shard_map/ppermute | solution.py:478
  36.6 7.1 %collective-permute-start.11 = (f32[264,128]{1,0:T(8,128)S(1)}, f32[264,128]{1,0:T(8,128)S(1)}, u32[]{:S(2)}, u32[]{:S(2)}) collective-permute-start(f32[264,128]{1,0:T(8,128)S(1)} %get-tuple-element.73), channel_id=1, source_target_pairs={{0,32},{32,0},{64,96},{96,64},{1,33},{33,1},{65,97},{97,65},{2,34}... | collective-permute-start | bytes 405512 | tf_op jit(solution)/shard_map/ppermute | solution.py:478
  43.7 4.7 %collective-permute-start.12 = (f32[72,128]{1,0:T(8,128)S(1)}, f32[72,128]{1,0:T(8,128)S(1)}, u32[]{:S(2)}, u32[]{:S(2)}) collective-permute-start(f32[72,128]{1,0:T(8,128)S(1)} %get-tuple-element.75), channel_id=1, source_target_pairs={{0,12},{4,8},{8,4},{12,0},{1,13},{5,9},{9,5},{13,1},{2,14},{6,10},... | collective-permute-start | bytes 110600 | tf_op jit(solution)/shard_map/ppermute | solution.py:478
  49.6 5.4 %collective-permute-start.15 = (f32[72,128]{1,0:T(8,128)S(1)}, f32[72,128]{1,0:T(8,128)S(1)}, u32[]{:S(2)}, u32[]{:S(2)}) collective-permute-start(f32[72,128]{1,0:T(8,128)S(1)} %fold_z.2.own), channel_id=1, source_target_pairs={{0,140},{4,136},{8,132},{12,128},{128,12},{132,8},{136,4},{140,0},... | collective-permute-start | bytes 110600 | tf_op jit(solution)/shard_map/ppermute | solution.py:478
  55.2 5.0 %collective-permute-start.18 = (f32[64,128]{1,0:T(8,128)S(1)}, f32[64,128]{1,0:T(8,128)S(1)}, u32[]{:S(2)}, u32[]{:S(2)}) collective-permute-start(f32[64,128]{1,0:T(8,128)S(1)} %update.2.traces), channel_id=1, source_target_pairs={{0,12},{4,8},{8,4},{12,0},{1,13},{5,9},{9,5},{13,1},{2,14},{6,10},... | collective-permute-start | bytes 98312 | tf_op jit(solution)/shard_map/ppermute | solution.py:478
  61.0 7.1 %collective-permute-start.21 = (f32[256,128]{1,0:T(8,128)S(1)}, f32[256,128]{1,0:T(8,128)S(1)}, u32[]{:S(2)}, u32[]{:S(2)}) collective-permute-start(f32[256,128]{1,0:T(8,128)S(1)} %pad_maximum_fusion.1), channel_id=1, source_target_pairs={{0,96},{32,64},{64,32},{96,0},{1,97},{33,65},{65,33},{97,1},{2,98}... | collective-permute-start | bytes 393224 | tf_op jit(solution)/shard_map/ppermute | solution.py:478
  61.9 6.3 %collective-permute-start.20 = (f32[256,128]{1,0:T(8,128)S(1)}, f32[256,128]{1,0:T(8,128)S(1)}, u32[]{:S(2)}, u32[]{:S(2)}) collective-permute-start(f32[256,128]{1,0:T(8,128)S(1)} %pad_maximum_fusion.1), channel_id=1, source_target_pairs={{0,64},{32,96},{64,0},{96,32},{1,65},{33,97},{65,1},{97,33},{2,66}... | collective-permute-start | bytes 393224 | tf_op jit(solution)/shard_map/ppermute | solution.py:478
  63.3 4.9 %collective-permute-start.19 = (f32[256,128]{1,0:T(8,128)S(1)}, f32[256,128]{1,0:T(8,128)S(1)}, u32[]{:S(2)}, u32[]{:S(2)}) collective-permute-start(f32[256,128]{1,0:T(8,128)S(1)} %pad_maximum_fusion.1), channel_id=1, source_target_pairs={{0,32},{32,0},{64,96},{96,64},{1,33},{33,1},{65,97},{97,65},{2,34}... | collective-permute-start | bytes 393224 | tf_op jit(solution)/shard_map/ppermute | solution.py:478
  68.2 8.4 %collective-permute-start.22 = (f32[1024,128]{1,0:T(8,128)S(1)}, f32[1024,128]{1,0:T(8,128)S(1)}, u32[]{:S(2)}, u32[]{:S(2)}) collective-permute-start(f32[1024,128]{1,0:T(8,128)S(1)} %constant_dynamic-update-slice_fusion.11.near), channel_id=1, source_target_pairs={{0,16},{16,0},{1,17},{17,1},{2,18},{18,2},{3,19},{19,3},{4,20},{20... | collective-permute-start | bytes 1572872 | tf_op jit(solution)/shard_map/ppermute | solution.py:478
  82.1 4.7 %collective-permute-start.24 = (f32[136,128]{1,0:T(8,128)S(1)}, f32[136,128]{1,0:T(8,128)S(1)}, u32[]{:S(2)}, u32[]{:S(2)}) collective-permute-start(f32[136,128]{1,0:T(8,128)S(1)} %get-tuple-element.81), channel_id=1, source_target_pairs={{0,2},{1,3},{2,0},{3,1},{4,6},{5,7},{6,4},{7,5},{8,10},{9,11},{10,... | collective-permute-start | bytes 208904 | tf_op jit(solution)/shard_map/ppermute | solution.py:478
  86.9 4.4 %collective-permute-start.28 = (f32[128,128]{1,0:T(8,128)S(1)}, f32[128,128]{1,0:T(8,128)S(1)}, u32[]{:S(2)}, u32[]{:S(2)}) collective-permute-start(f32[128,128]{1,0:T(8,128)S(1)} %step.2.foot), channel_id=1, source_target_pairs={{0,3},{1,2},{2,1},{3,0},{4,7},{5,6},{6,5},{7,4},{8,11},{9,10},{10,... | collective-permute-start | bytes 196616 | tf_op jit(solution)/shard_map/ppermute | solution.py:478
  87.9 4.6 %collective-permute-start.27 = (f32[128,128]{1,0:T(8,128)S(1)}, f32[128,128]{1,0:T(8,128)S(1)}, u32[]{:S(2)}, u32[]{:S(2)}) collective-permute-start(f32[128,128]{1,0:T(8,128)S(1)} %step.2.foot), channel_id=1, source_target_pairs={{0,2},{1,3},{2,0},{3,1},{4,6},{5,7},{6,4},{7,5},{8,10},{9,11},{10,... | collective-permute-start | bytes 196616 | tf_op jit(solution)/shard_map/ppermute | solution.py:478
  93.8 5.2 %collective-permute-start.29 = (f32[4,264,128]{2,1,0:T(8,128)S(1)}, f32[4,264,128]{2,1,0:T(8,128)S(1)}, u32[]{:S(2)}, u32[]{:S(2)}) collective-permute-start(f32[4,264,128]{2,1,0:T(8,128)S(1)} %get-tuple-element.93), channel_id=1, source_target_pairs={{0,16},{16,0},{1,17},{17,1},{2,18},{18,2},{3,19},{19,3},{4,20},{20... | collective-permute-start | bytes 1622024 | tf_op jit(solution)/shard_map/ppermute | solution.py:478
  99.1 8.6 %collective-permute-start.30 = (f32[264,128]{1,0:T(8,128)S(1)}, f32[264,128]{1,0:T(8,128)S(1)}, u32[]{:S(2)}, u32[]{:S(2)}) collective-permute-start(f32[264,128]{1,0:T(8,128)S(1)} %get-tuple-element.95), channel_id=1, source_target_pairs={{0,96},{32,64},{64,32},{96,0},{1,97},{33,65},{65,33},{97,1},{2,98}... | collective-permute-start | bytes 405512 | tf_op jit(solution)/shard_map/ppermute | solution.py:478
  100.1 7.6 %collective-permute-start.31 = (f32[264,128]{1,0:T(8,128)S(1)}, f32[264,128]{1,0:T(8,128)S(1)}, u32[]{:S(2)}, u32[]{:S(2)}) collective-permute-start(f32[264,128]{1,0:T(8,128)S(1)} %get-tuple-element.96), channel_id=1, source_target_pairs={{0,64},{32,96},{64,0},{96,32},{1,65},{33,97},{65,1},{97,33},{2,66}... | collective-permute-start | bytes 405512 | tf_op jit(solution)/shard_map/ppermute | solution.py:478
  101.3 7.1 %collective-permute-start.32 = (f32[264,128]{1,0:T(8,128)S(1)}, f32[264,128]{1,0:T(8,128)S(1)}, u32[]{:S(2)}, u32[]{:S(2)}) collective-permute-start(f32[264,128]{1,0:T(8,128)S(1)} %get-tuple-element.97), channel_id=1, source_target_pairs={{0,32},{32,0},{64,96},{96,64},{1,33},{33,1},{65,97},{97,65},{2,34}... | collective-permute-start | bytes 405512 | tf_op jit(solution)/shard_map/ppermute | solution.py:478
  108.5 4.7 %collective-permute-start.33 = (f32[72,128]{1,0:T(8,128)S(1)}, f32[72,128]{1,0:T(8,128)S(1)}, u32[]{:S(2)}, u32[]{:S(2)}) collective-permute-start(f32[72,128]{1,0:T(8,128)S(1)} %get-tuple-element.99), channel_id=1, source_target_pairs={{0,12},{4,8},{8,4},{12,0},{1,13},{5,9},{9,5},{13,1},{2,14},{6,10},... | collective-permute-start | bytes 110600 | tf_op jit(solution)/shard_map/ppermute | solution.py:478
  114.4 5.2 %collective-permute-start.36 = (f32[72,128]{1,0:T(8,128)S(1)}, f32[72,128]{1,0:T(8,128)S(1)}, u32[]{:S(2)}, u32[]{:S(2)}) collective-permute-start(f32[72,128]{1,0:T(8,128)S(1)} %fold_z.3.own), channel_id=1, source_target_pairs={{0,140},{4,136},{8,132},{12,128},{128,12},{132,8},{136,4},{140,0},... | collective-permute-start | bytes 110600 | tf_op jit(solution)/shard_map/ppermute | solution.py:478
  119.6 4.8 %collective-permute-start.39 = (f32[64,128]{1,0:T(8,128)S(1)}, f32[64,128]{1,0:T(8,128)S(1)}, u32[]{:S(2)}, u32[]{:S(2)}) collective-permute-start(f32[64,128]{1,0:T(8,128)S(1)} %update.3), channel_id=1, source_target_pairs={{0,12},{4,8},{8,4},{12,0},{1,13},{5,9},{9,5},{13,1},{2,14},{6,10},... | collective-permute-start | bytes 98312 | tf_op jit(solution)/shard_map/ppermute | solution.py:478
  125.7 7.1 %collective-permute-start.42 = (f32[256,128]{1,0:T(8,128)S(1)}, f32[256,128]{1,0:T(8,128)S(1)}, u32[]{:S(2)}, u32[]{:S(2)}) collective-permute-start(f32[256,128]{1,0:T(8,128)S(1)} %pad_maximum_fusion.2), channel_id=1, source_target_pairs={{0,96},{32,64},{64,32},{96,0},{1,97},{33,65},{65,33},{97,1},{2,98}... | collective-permute-start | bytes 393224 | tf_op jit(solution)/shard_map/ppermute | solution.py:478
  126.8 6.0 %collective-permute-start.41 = (f32[256,128]{1,0:T(8,128)S(1)}, f32[256,128]{1,0:T(8,128)S(1)}, u32[]{:S(2)}, u32[]{:S(2)}) collective-permute-start(f32[256,128]{1,0:T(8,128)S(1)} %pad_maximum_fusion.2), channel_id=1, source_target_pairs={{0,64},{32,96},{64,0},{96,32},{1,65},{33,97},{65,1},{97,33},{2,66}... | collective-permute-start | bytes 393224 | tf_op jit(solution)/shard_map/ppermute | solution.py:478
  128.2 4.6 %collective-permute-start.40 = (f32[256,128]{1,0:T(8,128)S(1)}, f32[256,128]{1,0:T(8,128)S(1)}, u32[]{:S(2)}, u32[]{:S(2)}) collective-permute-start(f32[256,128]{1,0:T(8,128)S(1)} %pad_maximum_fusion.2), channel_id=1, source_target_pairs={{0,32},{32,0},{64,96},{96,64},{1,33},{33,1},{65,97},{97,65},{2,34}... | collective-permute-start | bytes 393224 | tf_op jit(solution)/shard_map/ppermute | solution.py:478
  132.9 8.4 %collective-permute-start.43 = (f32[1024,128]{1,0:T(8,128)S(1)}, f32[1024,128]{1,0:T(8,128)S(1)}, u32[]{:S(2)}, u32[]{:S(2)}) collective-permute-start(f32[1024,128]{1,0:T(8,128)S(1)} %constant_dynamic-update-slice_fusion.18.near), channel_id=1, source_target_pairs={{0,16},{16,0},{1,17},{17,1},{2,18},{18,2},{3,19},{19,3},{4,20},{20... | collective-permute-start | bytes 1572872 | tf_op jit(solution)/shard_map/ppermute | solution.py:478
  145.7 4.8 %collective-permute-start.45 = (f32[136,128]{1,0:T(8,128)S(1)}, f32[136,128]{1,0:T(8,128)S(1)}, u32[]{:S(2)}, u32[]{:S(2)}) collective-permute-start(f32[136,128]{1,0:T(8,128)S(1)} %get-tuple-element.103), channel_id=1, source_target_pairs={{0,2},{1,3},{2,0},{3,1},{4,6},{5,7},{6,4},{7,5},{8,10},{9,11},{10,... | collective-permute-start | bytes 208904 | tf_op jit(solution)/shard_map/ppermute | solution.py:478
  152.2 4.6 %collective-permute-start.48 = (f32[128,128]{1,0:T(8,128)S(1)}, f32[128,128]{1,0:T(8,128)S(1)}, u32[]{:S(2)}, u32[]{:S(2)}) collective-permute-start(f32[128,128]{1,0:T(8,128)S(1)} %step.3.f0), channel_id=1, source_target_pairs={{0,2},{1,3},{2,0},{3,1},{4,6},{5,7},{6,4},{7,5},{8,10},{9,11},{10,... | collective-permute-start | bytes 196616 | tf_op jit(solution)/shard_map/ppermute | solution.py:478
  (18 other events, 68.0 us)

commit v2 on v1

--- a/solution.py
+++ b/solution.py
@@ -96,18 +96,16 @@
     return pl.ds(pl.multiple_of(g * 128, 128), 128)
 
 
-def first_kernel(
-    entry, movie, footprints, place, column, valid, foot, pairs, proj, gram, frames, came, got
-):
+def prepare_kernel(entry, footprints, place, column, valid, foot, got):
     zh, y, c, zl = (lax.axis_index(name) for name in BLOCKS)
     x = lax.axis_index("ta")
-    tall = GT * TILE
+    copies = []
     for k in range(NGROUP):
-        g = x ^ k
-        at = pl.ds(pl.multiple_of(g * 128, 128), 128)
-        pltpu.make_async_copy(footprints.at[at], foot.at[pl.ds(k * 128, 128)], got.at[k]).start()
-        at = pl.ds(pl.multiple_of(g * tall, tall), tall)
-        pltpu.make_async_copy(movie.at[at], frames.at[pl.ds(k * tall, tall)], came.at[k]).start()
+        at = pl.ds(pl.multiple_of((x ^ k) * 128, 128), 128)
+        copies.append(
+            pltpu.make_async_copy(footprints.at[at], foot.at[pl.ds(k * 128, 128)], got.at[k])
+        )
+        copies[-1].start()
     for k in range(NGROUP):
         s = slice(k * 128, (k + 1) * 128)
         comp = entry[x ^ k]
@@ -120,12 +118,40 @@
         at = as_column(index.astype(f32), 128)
         column[s, :] = at.astype(jnp.int32)
         valid[s, :] = jnp.where(at < K, 1.0, 0.0)
+    for k in range(NGROUP):
+        s = slice(k * 128, (k + 1) * 128)
+        copies[k].wait()
+        foot[s, :] = foot[s, :] * valid[s, :]
+
+
+def prepare(entry, footprints):
+    return pl.pallas_call(
+        prepare_kernel,
+        in_specs=[VM, HB],
+        out_specs=[VM] * 4,
+        out_shape=[
+            like(1, 512, dtype=jnp.int32),
+            like(512, 1, dtype=jnp.int32),
+            like(512, 1),
+            like(512, TILE),
+        ],
+        scratch_shapes=[pltpu.SemaphoreType.DMA((NGROUP,))],
+        compiler_params=PARAMS,
+        cost_estimate=cost(16 * 16 * 256 * 128),
+        name="prepare",
+    )(entry, pltpu.with_memory_space_constraint(footprints, pltpu.HBM))
+
+
+def first_kernel(movie, foot, pairs, proj, gram, frames, came):
+    x = lax.axis_index("ta")
+    tall = GT * TILE
+    for k in range(NGROUP):
+        at = pl.ds(pl.multiple_of((x ^ k) * tall, tall), tall)
+        pltpu.make_async_copy(movie.at[at], frames.at[pl.ds(k * tall, tall)], came.at[k]).start()
 
     def group(k, carry):
         s = rows_of(k)
-        pltpu.make_async_copy(footprints.at[s], foot.at[s], got.at[k]).wait()
-        f = foot[s, :] * valid[s, :]
-        foot[s, :] = f
+        f = foot[s, :]
         gram[k] = jnp.where(same_tile(), nt3(f, f), 0.0)
         at = pl.ds(pl.multiple_of(k * tall, tall), tall)
         pltpu.make_async_copy(movie.at[at], frames.at[at], came.at[k]).wait()
@@ -142,33 +168,21 @@
     lax.fori_loop(0, NGROUP, group, 0)
 
 
-def first(entry, movie, footprints):
+def first(movie, foot):
     return pl.pallas_call(
         first_kernel,
-        in_specs=[VM, HB, HB],
-        out_specs=[VM] * 7,
+        in_specs=[HB, VM],
+        out_specs=[VM] * 3,
         out_shape=[
-            like(1, 512, dtype=jnp.int32),
-            like(512, 1, dtype=jnp.int32),
-            like(512, 1),
-            like(512, TILE),
             pltpu.VMEM((64, 2 * TILE, 128), bf16),
             like(512, 128),
             like(NGROUP, 128, 128),
         ],
-        scratch_shapes=[
-            pltpu.VMEM((64 * TILE, 128), f32),
-            pltpu.SemaphoreType.DMA((NGROUP,)),
-            pltpu.SemaphoreType.DMA((NGROUP,)),
-        ],
+        scratch_shapes=[pltpu.VMEM((64 * TILE, 128), f32), pltpu.SemaphoreType.DMA((NGROUP,))],
         compiler_params=PARAMS,
         cost_estimate=cost(64 * 16 * 256 * 128),
         name="first",
-    )(
-        entry,
-        pltpu.with_memory_space_constraint(movie, pltpu.HBM),
-        pltpu.with_memory_space_constraint(footprints, pltpu.HBM),
-    )
+    )(pltpu.with_memory_space_constraint(movie, pltpu.HBM), foot)
 
 
 def scatter(half, place, both, curv, out, looped):
@@ -496,9 +510,9 @@
 
 
 def new_feet(column, near, far, foot, valid, pairs):
-    picked, piece = picked_gradient(2, column, pick_near(column, near), far, foot, pairs)
-    came = {2: swapped(piece, "ta", 2)}
-    for k in (1, 3):
+    picked, piece = picked_gradient(3, column, pick_near(column, near), far, foot, pairs)
+    came = {3: swapped(piece, "ta", 3)}
+    for k in (2, 1):
         piece = gradient(k, picked, foot, pairs)
         came[k] = swapped(piece, "ta", k)
     came[0] = gradient(0, picked, foot, pairs)
@@ -511,11 +525,11 @@
     twin, entry = lax.optimization_barrier((across(traces), entry))
     own = jnp.concatenate([traces, twin], axis=0)
     part = gathered(own, "zl")
-    made = first(entry, movie, footprints.reshape(-1, TILE))
-    part, place, column, valid, foot, pairs, proj, gram = lax.optimization_barrier(
-        (part, *made)
-    )
+    made = prepare(entry, footprints.reshape(-1, TILE))
+    part, place, column, valid, foot = lax.optimization_barrier((part, *made))
     near = gathered(part, "y")
+    made = first(movie, foot)
+    near, pairs, proj, gram = lax.optimization_barrier((near, *made))
     far = swapped(near, "c", 1)
     sums = numerators(place, column, proj, gram, pick_near(column, near), far)
     for step in range(ITERS):

time: 159 us -> 160 us (level)
    pallas_call x1 -> x2, Pallas kernels: 3.73 us -> 4.49 us  [the longest x1 3.25 us: first(): pl.pallas_call(first_kernel, in_specs=[HB, VM], out_specs=[VM] * 3, out_s...]
  transfers between devices with their start and end apart: 50 -> 50, of which waited for: 33 -> 36; matrix products, arithmetic and copies ran while one was open for 1% -> 1% of each run, Pallas kernels for 7% -> 7%
where the time goes in v2:
time: 160 us; the launch traced here: 158 us
  starting transfers between devices  84.7 us (53%)
  waiting for transfers between devices  49.5 us (31%)
  Pallas kernels  20.2 us (13%)
  local copies, waits for them, and re-layouts  2.34 us (1%)
    ppermute x50, starting transfers between devices, swapped(): return lax.ppermute(x, axis, [(i, i ^ bits) for i in range(n)])  84.7 us
    ppermute x50, waiting for transfers between devices, swapped(): return lax.ppermute(x, axis, [(i, i ^ bits) for i in range(n)])  49.5 us
    pallas_call x1, Pallas kernels, first(): pl.pallas_call(first_kernel, in_specs=[HB, VM], out_specs=[VM] * 3, out_s...  3.25 us
  transfers between devices with their start and end apart: 50, of which 36 were waited for; matrix products, arithmetic and copies ran while one was open for 1% of the time, Pallas kernels for 7%

profile of v2, /device:TPU:1, one launch (start us, length us, event | category | flops | bytes accessed | tf_op | source)
XLA Modules:
  0.0 157.9 jit_solution(15030493158860833380)
XLA Ops:
  0.6 6.5 %collective-permute-start = (f32[32,128]{1,0:T(8,128)}, f32[32,128]{1,0:T(8,128)S(1)}, u32[]{:S(2)}, u32[]{:S(2)}) collective-permute-start(f32[32,128]{1,0:T(8,128)} %param.5), channel_id=1, source_target_pairs={{0,140},{4,136},{8,132},{12,128},{128,12},{132,8},{136,4},{140,0},... | collective-permute-start | bytes 49160 | tf_op jit(solution)/shard_map/ppermute | solution.py:492
  8.7 1.7 %collective-permute-start.1 = (f32[64,128]{1,0:T(8,128)S(1)}, f32[64,128]{1,0:T(8,128)S(1)}, u32[]{:S(2)}, u32[]{:S(2)}) collective-permute-start(f32[64,128]{1,0:T(8,128)S(1)} %get-tuple-element.106.traces), channel_id=1, source_target_pairs={{0,4},{4,0},{8,12},{12,8},{1,5},{5,1},{9,13},{13,9},{2,6},{6,2},{1... | collective-permute-start | bytes 98312 | tf_op jit(solution)/shard_map/ppermute | solution.py:492
  10.5 1.6 %collective-permute-start.3 = (f32[64,128]{1,0:T(8,128)S(1)}, f32[64,128]{1,0:T(8,128)S(1)}, u32[]{:S(2)}, u32[]{:S(2)}) collective-permute-start(f32[64,128]{1,0:T(8,128)S(1)} %get-tuple-element.106.traces), channel_id=1, source_target_pairs={{0,12},{4,8},{8,4},{12,0},{1,13},{5,9},{9,5},{13,1},{2,14},{6,10},... | collective-permute-start | bytes 98312 | tf_op jit(solution)/shard_map/ppermute | solution.py:492
  13.4 2.7 %collective-permute-done.2 = f32[64,128]{1,0:T(8,128)S(1)} collective-permute-done((f32[64,128]{1,0:T(8,128)S(1)}, f32[64,128]{1,0:T(8,128)S(1)}, u32[]{:S(2)}, u32[]{:S(2)}) %collective-permute-start.2) | collective-permute-done | bytes 32800 | tf_op jit(solution)/shard_map/ppermute | solution.py:492
  16.1 2.8 %collective-permute-start.6 = (f32[256,128]{1,0:T(8,128)S(1)}, f32[256,128]{1,0:T(8,128)S(1)}, u32[]{:S(2)}, u32[]{:S(2)}) collective-permute-start(f32[256,128]{1,0:T(8,128)S(1)} %constant_dynamic-update-slice_fusion.2), channel_id=1, source_target_pairs={{0,96},{32,64},{64,32},{96,0},{1,97},{33,65},{65,33},{97,1},{2,98}... | collective-permute-start | bytes 393224 | tf_op jit(solution)/shard_map/ppermute | solution.py:492
  19.6 3.2 %first.1 = (bf16[64,256,128]{2,1,0:T(8,128)(2,1)S(1)}, f32[512,128]{1,0:T(8,128)S(1)}, f32[4,128,128]{2,1,0:T(8,128)S(1)}) custom-call(f32[8192,128]{1,0:T(8,128)} %movie.1, f32[512,128]{1,0:T(8,128)S(1)} %get-tuple-element.63.foot), custom_call_target="tpu_custom_call" | custom-call | flops 67108864 | bytes 1048576 | tf_op jit(solution)/shard_map/first/pallas_call | solution.py:172
  24.4 4.1 %collective-permute-start.7 = (f32[1024,128]{1,0:T(8,128)S(1)}, f32[1024,128]{1,0:T(8,128)S(1)}, u32[]{:S(2)}, u32[]{:S(2)}) collective-permute-start(f32[1024,128]{1,0:T(8,128)S(1)} %pad_maximum_fusion.near), channel_id=1, source_target_pairs={{0,16},{16,0},{1,17},{17,1},{2,18},{18,2},{3,19},{19,3},{4,20},{20... | collective-permute-start | bytes 1572872 | tf_op jit(solution)/shard_map/ppermute | solution.py:492
  33.5 1.8 %collective-permute-start.9 = (f32[264,128]{1,0:T(8,128)S(1)}, f32[264,128]{1,0:T(8,128)S(1)}, u32[]{:S(2)}, u32[]{:S(2)}) collective-permute-start(f32[264,128]{1,0:T(8,128)S(1)} %get-tuple-element.74), channel_id=1, source_target_pairs={{0,96},{32,64},{64,32},{96,0},{1,97},{33,65},{65,33},{97,1},{2,98}... | collective-permute-start | bytes 405512 | tf_op jit(solution)/shard_map/ppermute | solution.py:492
  36.9 3.1 %collective-permute-done.9.b = f32[264,128]{1,0:T(8,128)S(1)} collective-permute-done((f32[264,128]{1,0:T(8,128)S(1)}, f32[264,128]{1,0:T(8,128)S(1)}, u32[]{:S(2)}, u32[]{:S(2)}) %collective-permute-start.9) | collective-permute-done | bytes 135200 | tf_op jit(solution)/shard_map/ppermute | solution.py:492
  42.9 1.6 %collective-permute-start.12 = (f32[72,128]{1,0:T(8,128)S(1)}, f32[72,128]{1,0:T(8,128)S(1)}, u32[]{:S(2)}, u32[]{:S(2)}) collective-permute-start(f32[72,128]{1,0:T(8,128)S(1)} %get-tuple-element.78), channel_id=1, source_target_pairs={{0,12},{4,8},{8,4},{12,0},{1,13},{5,9},{9,5},{13,1},{2,14},{6,10},... | collective-permute-start | bytes 110600 | tf_op jit(solution)/shard_map/ppermute | solution.py:492
  44.6 2.0 %collective-permute-start.14 = (f32[72,128]{1,0:T(8,128)S(1)}, f32[72,128]{1,0:T(8,128)S(1)}, u32[]{:S(2)}, u32[]{:S(2)}) collective-permute-start(f32[72,128]{1,0:T(8,128)S(1)} %get-tuple-element.80), channel_id=1, source_target_pairs={{0,4},{4,0},{8,12},{12,8},{1,5},{5,1},{9,13},{13,9},{2,6},{6,2},{1... | collective-permute-start | bytes 110600 | tf_op jit(solution)/shard_map/ppermute | solution.py:492
  48.4 3.8 %collective-permute-start.15 = (f32[72,128]{1,0:T(8,128)S(1)}, f32[72,128]{1,0:T(8,128)S(1)}, u32[]{:S(2)}, u32[]{:S(2)}) collective-permute-start(f32[72,128]{1,0:T(8,128)S(1)} %fold_z.2.own), channel_id=1, source_target_pairs={{0,140},{4,136},{8,132},{12,128},{128,12},{132,8},{136,4},{140,0},... | collective-permute-start | bytes 110600 | tf_op jit(solution)/shard_map/ppermute | solution.py:492
  53.7 1.7 %collective-permute-start.18 = (f32[64,128]{1,0:T(8,128)S(1)}, f32[64,128]{1,0:T(8,128)S(1)}, u32[]{:S(2)}, u32[]{:S(2)}) collective-permute-start(f32[64,128]{1,0:T(8,128)S(1)} %update.2.traces), channel_id=1, source_target_pairs={{0,12},{4,8},{8,4},{12,0},{1,13},{5,9},{9,5},{13,1},{2,14},{6,10},... | collective-permute-start | bytes 98312 | tf_op jit(solution)/shard_map/ppermute | solution.py:492
  55.5 1.8 %collective-permute-start.17 = (f32[64,128]{1,0:T(8,128)S(1)}, f32[64,128]{1,0:T(8,128)S(1)}, u32[]{:S(2)}, u32[]{:S(2)}) collective-permute-start(f32[64,128]{1,0:T(8,128)S(1)} %update.2.traces), channel_id=1, source_target_pairs={{0,8},{4,12},{8,0},{12,4},{1,9},{5,13},{9,1},{13,5},{2,10},{6,14},... | collective-permute-start | bytes 98312 | tf_op jit(solution)/shard_map/ppermute | solution.py:492
  60.0 1.8 %collective-permute-start.21 = (f32[256,128]{1,0:T(8,128)S(1)}, f32[256,128]{1,0:T(8,128)S(1)}, u32[]{:S(2)}, u32[]{:S(2)}) collective-permute-start(f32[256,128]{1,0:T(8,128)S(1)} %pad_maximum_fusion.2), channel_id=1, source_target_pairs={{0,96},{32,64},{64,32},{96,0},{1,97},{33,65},{65,33},{97,1},{2,98}... | collective-permute-start | bytes 393224 | tf_op jit(solution)/shard_map/ppermute | solution.py:492
  63.4 3.8 %collective-permute-done.19 = f32[256,128]{1,0:T(8,128)S(1)} collective-permute-done((f32[256,128]{1,0:T(8,128)S(1)}, f32[256,128]{1,0:T(8,128)S(1)}, u32[]{:S(2)}, u32[]{:S(2)}) %collective-permute-start.19) | collective-permute-done | bytes 131104 | tf_op jit(solution)/shard_map/ppermute | solution.py:492
  67.2 6.9 %collective-permute-start.22 = (f32[1024,128]{1,0:T(8,128)S(1)}, f32[1024,128]{1,0:T(8,128)S(1)}, u32[]{:S(2)}, u32[]{:S(2)}) collective-permute-start(f32[1024,128]{1,0:T(8,128)S(1)} %constant_dynamic-update-slice_fusion.7.near), channel_id=1, source_target_pairs={{0,16},{16,0},{1,17},{17,1},{2,18},{18,2},{3,19},{19,3},{4,20},{20... | collective-permute-start | bytes 1572872 | tf_op jit(solution)/shard_map/ppermute | solution.py:492
  79.5 2.4 %collective-permute-start.24 = (f32[136,128]{1,0:T(8,128)S(1)}, f32[136,128]{1,0:T(8,128)S(1)}, u32[]{:S(2)}, u32[]{:S(2)}) collective-permute-start(f32[136,128]{1,0:T(8,128)S(1)} %gradient.8), channel_id=1, source_target_pairs={{0,2},{1,3},{2,0},{3,1},{4,6},{5,7},{6,4},{7,5},{8,10},{9,11},{10,... | collective-permute-start | bytes 208904 | tf_op jit(solution)/shard_map/ppermute | solution.py:492
  82.7 2.4 %collective-permute-done.24.c = f32[136,128]{1,0:T(8,128)S(1)} collective-permute-done((f32[136,128]{1,0:T(8,128)S(1)}, f32[136,128]{1,0:T(8,128)S(1)}, u32[]{:S(2)}, u32[]{:S(2)}) %collective-permute-start.24) | collective-permute-done | bytes 69664 | tf_op jit(solution)/shard_map/ppermute | solution.py:492
  85.0 1.6 %collective-permute-done.25.d = f32[136,128]{1,0:T(8,128)S(1)} collective-permute-done((f32[136,128]{1,0:T(8,128)S(1)}, f32[136,128]{1,0:T(8,128)S(1)}, u32[]{:S(2)}, u32[]{:S(2)}) %collective-permute-start.25) | collective-permute-done | bytes 69664 | tf_op jit(solution)/shard_map/ppermute | solution.py:492
  94.2 2.4 %collective-permute-start.29 = (f32[4,264,128]{2,1,0:T(8,128)S(1)}, f32[4,264,128]{2,1,0:T(8,128)S(1)}, u32[]{:S(2)}, u32[]{:S(2)}) collective-permute-start(f32[4,264,128]{2,1,0:T(8,128)S(1)} %get-tuple-element.95), channel_id=1, source_target_pairs={{0,16},{16,0},{1,17},{17,1},{2,18},{18,2},{3,19},{19,3},{4,20},{20... | collective-permute-start | bytes 1622024 | tf_op jit(solution)/shard_map/ppermute | solution.py:492
  98.3 1.8 %collective-permute-start.30 = (f32[264,128]{1,0:T(8,128)S(1)}, f32[264,128]{1,0:T(8,128)S(1)}, u32[]{:S(2)}, u32[]{:S(2)}) collective-permute-start(f32[264,128]{1,0:T(8,128)S(1)} %get-tuple-element.97), channel_id=1, source_target_pairs={{0,96},{32,64},{64,32},{96,0},{1,97},{33,65},{65,33},{97,1},{2,98}... | collective-permute-start | bytes 405512 | tf_op jit(solution)/shard_map/ppermute | solution.py:492
  101.6 3.1 %collective-permute-done.30.b = f32[264,128]{1,0:T(8,128)S(1)} collective-permute-done((f32[264,128]{1,0:T(8,128)S(1)}, f32[264,128]{1,0:T(8,128)S(1)}, u32[]{:S(2)}, u32[]{:S(2)}) %collective-permute-start.30) | collective-permute-done | bytes 135200 | tf_op jit(solution)/shard_map/ppermute | solution.py:492
  107.7 1.6 %collective-permute-start.33 = (f32[72,128]{1,0:T(8,128)S(1)}, f32[72,128]{1,0:T(8,128)S(1)}, u32[]{:S(2)}, u32[]{:S(2)}) collective-permute-start(f32[72,128]{1,0:T(8,128)S(1)} %get-tuple-element.101), channel_id=1, source_target_pairs={{0,12},{4,8},{8,4},{12,0},{1,13},{5,9},{9,5},{13,1},{2,14},{6,10},... | collective-permute-start | bytes 110600 | tf_op jit(solution)/shard_map/ppermute | solution.py:492
  109.3 2.0 %collective-permute-start.35 = (f32[72,128]{1,0:T(8,128)S(1)}, f32[72,128]{1,0:T(8,128)S(1)}, u32[]{:S(2)}, u32[]{:S(2)}) collective-permute-start(f32[72,128]{1,0:T(8,128)S(1)} %get-tuple-element.103), channel_id=1, source_target_pairs={{0,4},{4,0},{8,12},{12,8},{1,5},{5,1},{9,13},{13,9},{2,6},{6,2},{1... | collective-permute-start | bytes 110600 | tf_op jit(solution)/shard_map/ppermute | solution.py:492
  113.6 4.2 %collective-permute-start.36 = (f32[72,128]{1,0:T(8,128)S(1)}, f32[72,128]{1,0:T(8,128)S(1)}, u32[]{:S(2)}, u32[]{:S(2)}) collective-permute-start(f32[72,128]{1,0:T(8,128)S(1)} %fold_z.3.own), channel_id=1, source_target_pairs={{0,140},{4,136},{8,132},{12,128},{128,12},{132,8},{136,4},{140,0},... | collective-permute-start | bytes 110600 | tf_op jit(solution)/shard_map/ppermute | solution.py:492
  119.2 1.7 %collective-permute-start.39 = (f32[64,128]{1,0:T(8,128)S(1)}, f32[64,128]{1,0:T(8,128)S(1)}, u32[]{:S(2)}, u32[]{:S(2)}) collective-permute-start(f32[64,128]{1,0:T(8,128)S(1)} %update.3), channel_id=1, source_target_pairs={{0,12},{4,8},{8,4},{12,0},{1,13},{5,9},{9,5},{13,1},{2,14},{6,10},... | collective-permute-start | bytes 98312 | tf_op jit(solution)/shard_map/ppermute | solution.py:492
  125.1 1.8 %collective-permute-start.42 = (f32[256,128]{1,0:T(8,128)S(1)}, f32[256,128]{1,0:T(8,128)S(1)}, u32[]{:S(2)}, u32[]{:S(2)}) collective-permute-start(f32[256,128]{1,0:T(8,128)S(1)} %pad_maximum_fusion.3), channel_id=1, source_target_pairs={{0,96},{32,64},{64,32},{96,0},{1,97},{33,65},{65,33},{97,1},{2,98}... | collective-permute-start | bytes 393224 | tf_op jit(solution)/shard_map/ppermute | solution.py:492
  128.5 3.8 %collective-permute-done.40 = f32[256,128]{1,0:T(8,128)S(1)} collective-permute-done((f32[256,128]{1,0:T(8,128)S(1)}, f32[256,128]{1,0:T(8,128)S(1)}, u32[]{:S(2)}, u32[]{:S(2)}) %collective-permute-start.40) | collective-permute-done | bytes 131104 | tf_op jit(solution)/shard_map/ppermute | solution.py:492
  132.3 7.0 %collective-permute-start.43 = (f32[1024,128]{1,0:T(8,128)S(1)}, f32[1024,128]{1,0:T(8,128)S(1)}, u32[]{:S(2)}, u32[]{:S(2)}) collective-permute-start(f32[1024,128]{1,0:T(8,128)S(1)} %constant_dynamic-update-slice_fusion.14.near), channel_id=1, source_target_pairs={{0,16},{16,0},{1,17},{17,1},{2,18},{18,2},{3,19},{19,3},{4,20},{20... | collective-permute-start | bytes 1572872 | tf_op jit(solution)/shard_map/ppermute | solution.py:492
  144.4 2.2 %collective-permute-start.45 = (f32[136,128]{1,0:T(8,128)S(1)}, f32[136,128]{1,0:T(8,128)S(1)}, u32[]{:S(2)}, u32[]{:S(2)}) collective-permute-start(f32[136,128]{1,0:T(8,128)S(1)} %gradient.11), channel_id=1, source_target_pairs={{0,2},{1,3},{2,0},{3,1},{4,6},{5,7},{6,4},{7,5},{8,10},{9,11},{10,... | collective-permute-start | bytes 208904 | tf_op jit(solution)/shard_map/ppermute | solution.py:492
  147.7 2.0 %collective-permute-done.45.c = f32[136,128]{1,0:T(8,128)S(1)} collective-permute-done((f32[136,128]{1,0:T(8,128)S(1)}, f32[136,128]{1,0:T(8,128)S(1)}, u32[]{:S(2)}, u32[]{:S(2)}) %collective-permute-start.45) | collective-permute-done | bytes 69664 | tf_op jit(solution)/shard_map/ppermute | solution.py:492
  (126 shorter events, 65.9 us)
Async XLA Ops:
  0.6 8.1 %collective-permute-start = (f32[32,128]{1,0:T(8,128)}, f32[32,128]{1,0:T(8,128)S(1)}, u32[]{:S(2)}, u32[]{:S(2)}) collective-permute-start(f32[32,128]{1,0:T(8,128)} %param.5), channel_id=1, source_target_pairs={{0,140},{4,136},{8,132},{12,128},{128,12},{132,8},{136,4},{140,0},... | collective-permute-start | bytes 49160 | tf_op jit(solution)/shard_map/ppermute | solution.py:492
  10.5 5.6 %collective-permute-start.3 = (f32[64,128]{1,0:T(8,128)S(1)}, f32[64,128]{1,0:T(8,128)S(1)}, u32[]{:S(2)}, u32[]{:S(2)}) collective-permute-start(f32[64,128]{1,0:T(8,128)S(1)} %get-tuple-element.106.traces), channel_id=1, source_target_pairs={{0,12},{4,8},{8,4},{12,0},{1,13},{5,9},{9,5},{13,1},{2,14},{6,10},... | collective-permute-start | bytes 98312 | tf_op jit(solution)/shard_map/ppermute | solution.py:492
  16.1 6.8 %collective-permute-start.6 = (f32[256,128]{1,0:T(8,128)S(1)}, f32[256,128]{1,0:T(8,128)S(1)}, u32[]{:S(2)}, u32[]{:S(2)}) collective-permute-start(f32[256,128]{1,0:T(8,128)S(1)} %constant_dynamic-update-slice_fusion.2), channel_id=1, source_target_pairs={{0,96},{32,64},{64,32},{96,0},{1,97},{33,65},{65,33},{97,1},{2,98}... | collective-permute-start | bytes 393224 | tf_op jit(solution)/shard_map/ppermute | solution.py:492
  18.9 5.4 %collective-permute-start.5 = (f32[256,128]{1,0:T(8,128)S(1)}, f32[256,128]{1,0:T(8,128)S(1)}, u32[]{:S(2)}, u32[]{:S(2)}) collective-permute-start(f32[256,128]{1,0:T(8,128)S(1)} %constant_dynamic-update-slice_fusion.2), channel_id=1, source_target_pairs={{0,64},{32,96},{64,0},{96,32},{1,65},{33,97},{65,1},{97,33},{2,66}... | collective-permute-start | bytes 393224 | tf_op jit(solution)/shard_map/ppermute | solution.py:492
  19.2 5.1 %collective-permute-start.4 = (f32[256,128]{1,0:T(8,128)S(1)}, f32[256,128]{1,0:T(8,128)S(1)}, u32[]{:S(2)}, u32[]{:S(2)}) collective-permute-start(f32[256,128]{1,0:T(8,128)S(1)} %constant_dynamic-update-slice_fusion.2), channel_id=1, source_target_pairs={{0,32},{32,0},{64,96},{96,64},{1,33},{33,1},{65,97},{97,65},{2,34}... | collective-permute-start | bytes 393224 | tf_op jit(solution)/shard_map/ppermute | solution.py:492
  24.4 5.6 %collective-permute-start.7 = (f32[1024,128]{1,0:T(8,128)S(1)}, f32[1024,128]{1,0:T(8,128)S(1)}, u32[]{:S(2)}, u32[]{:S(2)}) collective-permute-start(f32[1024,128]{1,0:T(8,128)S(1)} %pad_maximum_fusion.near), channel_id=1, source_target_pairs={{0,16},{16,0},{1,17},{17,1},{2,18},{18,2},{3,19},{19,3},{4,20},{20... | collective-permute-start | bytes 1572872 | tf_op jit(solution)/shard_map/ppermute | solution.py:492
  33.5 6.4 %collective-permute-start.9 = (f32[264,128]{1,0:T(8,128)S(1)}, f32[264,128]{1,0:T(8,128)S(1)}, u32[]{:S(2)}, u32[]{:S(2)}) collective-permute-start(f32[264,128]{1,0:T(8,128)S(1)} %get-tuple-element.74), channel_id=1, source_target_pairs={{0,96},{32,64},{64,32},{96,0},{1,97},{33,65},{65,33},{97,1},{2,98}... | collective-permute-start | bytes 405512 | tf_op jit(solution)/shard_map/ppermute | solution.py:492
  35.3 6.1 %collective-permute-start.10 = (f32[264,128]{1,0:T(8,128)S(1)}, f32[264,128]{1,0:T(8,128)S(1)}, u32[]{:S(2)}, u32[]{:S(2)}) collective-permute-start(f32[264,128]{1,0:T(8,128)S(1)} %get-tuple-element.75), channel_id=1, source_target_pairs={{0,64},{32,96},{64,0},{96,32},{1,65},{33,97},{65,1},{97,33},{2,66}... | collective-permute-start | bytes 405512 | tf_op jit(solution)/shard_map/ppermute | solution.py:492
  35.7 7.2 %collective-permute-start.11 = (f32[264,128]{1,0:T(8,128)S(1)}, f32[264,128]{1,0:T(8,128)S(1)}, u32[]{:S(2)}, u32[]{:S(2)}) collective-permute-start(f32[264,128]{1,0:T(8,128)S(1)} %get-tuple-element.76), channel_id=1, source_target_pairs={{0,32},{32,0},{64,96},{96,64},{1,33},{33,1},{65,97},{97,65},{2,34}... | collective-permute-start | bytes 405512 | tf_op jit(solution)/shard_map/ppermute | solution.py:492
  42.9 4.7 %collective-permute-start.12 = (f32[72,128]{1,0:T(8,128)S(1)}, f32[72,128]{1,0:T(8,128)S(1)}, u32[]{:S(2)}, u32[]{:S(2)}) collective-permute-start(f32[72,128]{1,0:T(8,128)S(1)} %get-tuple-element.78), channel_id=1, source_target_pairs={{0,12},{4,8},{8,4},{12,0},{1,13},{5,9},{9,5},{13,1},{2,14},{6,10},... | collective-permute-start | bytes 110600 | tf_op jit(solution)/shard_map/ppermute | solution.py:492
  48.4 5.2 %collective-permute-start.15 = (f32[72,128]{1,0:T(8,128)S(1)}, f32[72,128]{1,0:T(8,128)S(1)}, u32[]{:S(2)}, u32[]{:S(2)}) collective-permute-start(f32[72,128]{1,0:T(8,128)S(1)} %fold_z.2.own), channel_id=1, source_target_pairs={{0,140},{4,136},{8,132},{12,128},{128,12},{132,8},{136,4},{140,0},... | collective-permute-start | bytes 110600 | tf_op jit(solution)/shard_map/ppermute | solution.py:492
  53.7 4.7 %collective-permute-start.18 = (f32[64,128]{1,0:T(8,128)S(1)}, f32[64,128]{1,0:T(8,128)S(1)}, u32[]{:S(2)}, u32[]{:S(2)}) collective-permute-start(f32[64,128]{1,0:T(8,128)S(1)} %update.2.traces), channel_id=1, source_target_pairs={{0,12},{4,8},{8,4},{12,0},{1,13},{5,9},{9,5},{13,1},{2,14},{6,10},... | collective-permute-start | bytes 98312 | tf_op jit(solution)/shard_map/ppermute | solution.py:492
  60.0 7.2 %collective-permute-start.21 = (f32[256,128]{1,0:T(8,128)S(1)}, f32[256,128]{1,0:T(8,128)S(1)}, u32[]{:S(2)}, u32[]{:S(2)}) collective-permute-start(f32[256,128]{1,0:T(8,128)S(1)} %pad_maximum_fusion.2), channel_id=1, source_target_pairs={{0,96},{32,64},{64,32},{96,0},{1,97},{33,65},{65,33},{97,1},{2,98}... | collective-permute-start | bytes 393224 | tf_op jit(solution)/shard_map/ppermute | solution.py:492
  61.8 5.4 %collective-permute-start.20 = (f32[256,128]{1,0:T(8,128)S(1)}, f32[256,128]{1,0:T(8,128)S(1)}, u32[]{:S(2)}, u32[]{:S(2)}) collective-permute-start(f32[256,128]{1,0:T(8,128)S(1)} %pad_maximum_fusion.2), channel_id=1, source_target_pairs={{0,64},{32,96},{64,0},{96,32},{1,65},{33,97},{65,1},{97,33},{2,66}... | collective-permute-start | bytes 393224 | tf_op jit(solution)/shard_map/ppermute | solution.py:492
  62.1 5.0 %collective-permute-start.19 = (f32[256,128]{1,0:T(8,128)S(1)}, f32[256,128]{1,0:T(8,128)S(1)}, u32[]{:S(2)}, u32[]{:S(2)}) collective-permute-start(f32[256,128]{1,0:T(8,128)S(1)} %pad_maximum_fusion.2), channel_id=1, source_target_pairs={{0,32},{32,0},{64,96},{96,64},{1,33},{33,1},{65,97},{97,65},{2,34}... | collective-permute-start | bytes 393224 | tf_op jit(solution)/shard_map/ppermute | solution.py:492
  67.2 8.5 %collective-permute-start.22 = (f32[1024,128]{1,0:T(8,128)S(1)}, f32[1024,128]{1,0:T(8,128)S(1)}, u32[]{:S(2)}, u32[]{:S(2)}) collective-permute-start(f32[1024,128]{1,0:T(8,128)S(1)} %constant_dynamic-update-slice_fusion.7.near), channel_id=1, source_target_pairs={{0,16},{16,0},{1,17},{17,1},{2,18},{18,2},{3,19},{19,3},{4,20},{20... | collective-permute-start | bytes 1572872 | tf_op jit(solution)/shard_map/ppermute | solution.py:492
  79.5 5.5 %collective-permute-start.24 = (f32[136,128]{1,0:T(8,128)S(1)}, f32[136,128]{1,0:T(8,128)S(1)}, u32[]{:S(2)}, u32[]{:S(2)}) collective-permute-start(f32[136,128]{1,0:T(8,128)S(1)} %gradient.8), channel_id=1, source_target_pairs={{0,2},{1,3},{2,0},{3,1},{4,6},{5,7},{6,4},{7,5},{8,10},{9,11},{10,... | collective-permute-start | bytes 208904 | tf_op jit(solution)/shard_map/ppermute | solution.py:492
  81.9 4.7 %collective-permute-start.25 = (f32[136,128]{1,0:T(8,128)S(1)}, f32[136,128]{1,0:T(8,128)S(1)}, u32[]{:S(2)}, u32[]{:S(2)}) collective-permute-start(f32[136,128]{1,0:T(8,128)S(1)} %get-tuple-element.83), channel_id=1, source_target_pairs={{0,3},{1,2},{2,1},{3,0},{4,7},{5,6},{6,5},{7,4},{8,11},{9,10},{10,... | collective-permute-start | bytes 208904 | tf_op jit(solution)/shard_map/ppermute | solution.py:492
  88.3 4.6 %collective-permute-start.27 = (f32[128,128]{1,0:T(8,128)S(1)}, f32[128,128]{1,0:T(8,128)S(1)}, u32[]{:S(2)}, u32[]{:S(2)}) collective-permute-start(f32[128,128]{1,0:T(8,128)S(1)} %step.2.foot), channel_id=1, source_target_pairs={{0,2},{1,3},{2,0},{3,1},{4,6},{5,7},{6,4},{7,5},{8,10},{9,11},{10,... | collective-permute-start | bytes 196616 | tf_op jit(solution)/shard_map/ppermute | solution.py:492
  98.3 6.4 %collective-permute-start.30 = (f32[264,128]{1,0:T(8,128)S(1)}, f32[264,128]{1,0:T(8,128)S(1)}, u32[]{:S(2)}, u32[]{:S(2)}) collective-permute-start(f32[264,128]{1,0:T(8,128)S(1)} %get-tuple-element.97), channel_id=1, source_target_pairs={{0,96},{32,64},{64,32},{96,0},{1,97},{33,65},{65,33},{97,1},{2,98}... | collective-permute-start | bytes 405512 | tf_op jit(solution)/shard_map/ppermute | solution.py:492
  100.0 6.1 %collective-permute-start.31 = (f32[264,128]{1,0:T(8,128)S(1)}, f32[264,128]{1,0:T(8,128)S(1)}, u32[]{:S(2)}, u32[]{:S(2)}) collective-permute-start(f32[264,128]{1,0:T(8,128)S(1)} %get-tuple-element.98), channel_id=1, source_target_pairs={{0,64},{32,96},{64,0},{96,32},{1,65},{33,97},{65,1},{97,33},{2,66}... | collective-permute-start | bytes 405512 | tf_op jit(solution)/shard_map/ppermute | solution.py:492
  100.5 7.1 %collective-permute-start.32 = (f32[264,128]{1,0:T(8,128)S(1)}, f32[264,128]{1,0:T(8,128)S(1)}, u32[]{:S(2)}, u32[]{:S(2)}) collective-permute-start(f32[264,128]{1,0:T(8,128)S(1)} %get-tuple-element.99), channel_id=1, source_target_pairs={{0,32},{32,0},{64,96},{96,64},{1,33},{33,1},{65,97},{97,65},{2,34}... | collective-permute-start | bytes 405512 | tf_op jit(solution)/shard_map/ppermute | solution.py:492
  107.7 4.7 %collective-permute-start.33 = (f32[72,128]{1,0:T(8,128)S(1)}, f32[72,128]{1,0:T(8,128)S(1)}, u32[]{:S(2)}, u32[]{:S(2)}) collective-permute-start(f32[72,128]{1,0:T(8,128)S(1)} %get-tuple-element.101), channel_id=1, source_target_pairs={{0,12},{4,8},{8,4},{12,0},{1,13},{5,9},{9,5},{13,1},{2,14},{6,10},... | collective-permute-start | bytes 110600 | tf_op jit(solution)/shard_map/ppermute | solution.py:492
  113.6 5.5 %collective-permute-start.36 = (f32[72,128]{1,0:T(8,128)S(1)}, f32[72,128]{1,0:T(8,128)S(1)}, u32[]{:S(2)}, u32[]{:S(2)}) collective-permute-start(f32[72,128]{1,0:T(8,128)S(1)} %fold_z.3.own), channel_id=1, source_target_pairs={{0,140},{4,136},{8,132},{12,128},{128,12},{132,8},{136,4},{140,0},... | collective-permute-start | bytes 110600 | tf_op jit(solution)/shard_map/ppermute | solution.py:492
  119.2 5.0 %collective-permute-start.39 = (f32[64,128]{1,0:T(8,128)S(1)}, f32[64,128]{1,0:T(8,128)S(1)}, u32[]{:S(2)}, u32[]{:S(2)}) collective-permute-start(f32[64,128]{1,0:T(8,128)S(1)} %update.3), channel_id=1, source_target_pairs={{0,12},{4,8},{8,4},{12,0},{1,13},{5,9},{9,5},{13,1},{2,14},{6,10},... | collective-permute-start | bytes 98312 | tf_op jit(solution)/shard_map/ppermute | solution.py:492
  125.1 7.2 %collective-permute-start.42 = (f32[256,128]{1,0:T(8,128)S(1)}, f32[256,128]{1,0:T(8,128)S(1)}, u32[]{:S(2)}, u32[]{:S(2)}) collective-permute-start(f32[256,128]{1,0:T(8,128)S(1)} %pad_maximum_fusion.3), channel_id=1, source_target_pairs={{0,96},{32,64},{64,32},{96,0},{1,97},{33,65},{65,33},{97,1},{2,98}... | collective-permute-start | bytes 393224 | tf_op jit(solution)/shard_map/ppermute | solution.py:492
  126.9 5.4 %collective-permute-start.41 = (f32[256,128]{1,0:T(8,128)S(1)}, f32[256,128]{1,0:T(8,128)S(1)}, u32[]{:S(2)}, u32[]{:S(2)}) collective-permute-start(f32[256,128]{1,0:T(8,128)S(1)} %pad_maximum_fusion.3), channel_id=1, source_target_pairs={{0,64},{32,96},{64,0},{96,32},{1,65},{33,97},{65,1},{97,33},{2,66}... | collective-permute-start | bytes 393224 | tf_op jit(solution)/shard_map/ppermute | solution.py:492
  127.3 4.9 %collective-permute-start.40 = (f32[256,128]{1,0:T(8,128)S(1)}, f32[256,128]{1,0:T(8,128)S(1)}, u32[]{:S(2)}, u32[]{:S(2)}) collective-permute-start(f32[256,128]{1,0:T(8,128)S(1)} %pad_maximum_fusion.3), channel_id=1, source_target_pairs={{0,32},{32,0},{64,96},{96,64},{1,33},{33,1},{65,97},{97,65},{2,34}... | collective-permute-start | bytes 393224 | tf_op jit(solution)/shard_map/ppermute | solution.py:492
  132.3 8.5 %collective-permute-start.43 = (f32[1024,128]{1,0:T(8,128)S(1)}, f32[1024,128]{1,0:T(8,128)S(1)}, u32[]{:S(2)}, u32[]{:S(2)}) collective-permute-start(f32[1024,128]{1,0:T(8,128)S(1)} %constant_dynamic-update-slice_fusion.14.near), channel_id=1, source_target_pairs={{0,16},{16,0},{1,17},{17,1},{2,18},{18,2},{3,19},{19,3},{4,20},{20... | collective-permute-start | bytes 1572872 | tf_op jit(solution)/shard_map/ppermute | solution.py:492
  144.4 5.3 %collective-permute-start.45 = (f32[136,128]{1,0:T(8,128)S(1)}, f32[136,128]{1,0:T(8,128)S(1)}, u32[]{:S(2)}, u32[]{:S(2)}) collective-permute-start(f32[136,128]{1,0:T(8,128)S(1)} %gradient.11), channel_id=1, source_target_pairs={{0,2},{1,3},{2,0},{3,1},{4,6},{5,7},{6,4},{7,5},{8,10},{9,11},{10,... | collective-permute-start | bytes 208904 | tf_op jit(solution)/shard_map/ppermute | solution.py:492
  146.6 4.7 %collective-permute-start.46 = (f32[136,128]{1,0:T(8,128)S(1)}, f32[136,128]{1,0:T(8,128)S(1)}, u32[]{:S(2)}, u32[]{:S(2)}) collective-permute-start(f32[136,128]{1,0:T(8,128)S(1)} %get-tuple-element.105), channel_id=1, source_target_pairs={{0,3},{1,2},{2,1},{3,0},{4,7},{5,6},{6,5},{7,4},{8,11},{9,10},{10,... | collective-permute-start | bytes 208904 | tf_op jit(solution)/shard_map/ppermute | solution.py:492
  152.2 4.6 %collective-permute-start.48 = (f32[128,128]{1,0:T(8,128)S(1)}, f32[128,128]{1,0:T(8,128)S(1)}, u32[]{:S(2)}, u32[]{:S(2)}) collective-permute-start(f32[128,128]{1,0:T(8,128)S(1)} %step.3.f0), channel_id=1, source_target_pairs={{0,2},{1,3},{2,0},{3,1},{4,6},{5,7},{6,4},{7,5},{8,10},{9,11},{10,... | collective-permute-start | bytes 196616 | tf_op jit(solution)/shard_map/ppermute | solution.py:492
  (18 other events, 69.7 us)

commit v3 on v2

--- a/solution.py
+++ b/solution.py
@@ -500,7 +500,7 @@
     came = swapped(other, "c", 1)
     ys = fold_core(scatter_mine(place, both, curv), came)
     zs = fold_y([ys[0]] + [swapped(ys[k], "y", k) for k in (3, 2, 1)])
-    own = fold_z([zs[0]] + [swapped(zs[k], "zl", k) for k in (3, 2, 1)])
+    own = fold_z([zs[0]] + [swapped(zs[k], "zl", k) for k in (2, 3, 1)])
     return own, across(own)
 
 
@@ -522,8 +522,7 @@
 
 def local(movie, traces, entry_comp, footprints):
     entry = entry_comp.reshape(NGROUP, 1, 128)
-    twin, entry = lax.optimization_barrier((across(traces), entry))
-    own = jnp.concatenate([traces, twin], axis=0)
+    own = jnp.concatenate([traces, across(traces)], axis=0)
     part = gathered(own, "zl")
     made = prepare(entry, footprints.reshape(-1, TILE))
     part, place, column, valid, foot = lax.optimization_barrier((part, *made))
@@ -534,7 +533,8 @@
     sums = numerators(place, column, proj, gram, pick_near(column, near), far)
     for step in range(ITERS):
         own = update(*summed_blocks(place, *sums), own)
-        near = gathered(gathered(own, "zl"), "y")
+        near = gathered(own, "zl")
+        near = gathered(near, "y")
         far = swapped(near, "c", 1)
         feet, picked = new_feet(column, near, far, foot, valid, pairs)
         if step + 1 < ITERS:

time: 160 us -> 161 us (level)
  waiting for transfers between devices: 49.5 us -> 53.2 us
  starting transfers between devices: 84.7 us -> 82.2 us
    ppermute x50, waiting for transfers between devices: 49.5 us -> 53.2 us  [swapped(): return lax.ppermute(x, axis, [(i, i ^ bits) for i in range(n)])]
    ppermute x50, starting transfers between devices: 84.7 us -> 82.2 us  [swapped(): return lax.ppermute(x, axis, [(i, i ^ bits) for i in range(n)])]
  transfers between devices with their start and end apart: 50 -> 50, of which waited for: 36 -> 38; matrix products, arithmetic and copies ran while one was open for 1% -> 1% of each run, Pallas kernels for 7% -> 7%
where the time goes in v3:
time: 161 us; the launch traced here: 159 us
  starting transfers between devices  82.2 us (51%)
  waiting for transfers between devices  53.2 us (33%)
  Pallas kernels  20.3 us (13%)
  local copies, waits for them, and re-layouts  2.33 us (1%)
    ppermute x50, starting transfers between devices, swapped(): return lax.ppermute(x, axis, [(i, i ^ bits) for i in range(n)])  82.2 us
    ppermute x50, waiting for transfers between devices, swapped(): return lax.ppermute(x, axis, [(i, i ^ bits) for i in range(n)])  53.2 us
    pallas_call x1, Pallas kernels, first(): pl.pallas_call(first_kernel, in_specs=[HB, VM], out_specs=[VM] * 3, out_s...  3.25 us
  transfers between devices with their start and end apart: 50, of which 38 were waited for; matrix products, arithmetic and copies ran while one was open for 1% of the time, Pallas kernels for 7%

profile of v3, /device:TPU:1, one launch (start us, length us, event | category | flops | bytes accessed | tf_op | source)
XLA Modules:
  0.0 159.1 jit_solution(5086193835424068998)
XLA Ops:
  0.6 6.5 %collective-permute-start = (f32[32,128]{1,0:T(8,128)}, f32[32,128]{1,0:T(8,128)S(1)}, u32[]{:S(2)}, u32[]{:S(2)}) collective-permute-start(f32[32,128]{1,0:T(8,128)} %param.5), channel_id=1, source_target_pairs={{0,140},{4,136},{8,132},{12,128},{128,12},{132,8},{136,4},{140,0},... | collective-permute-start | bytes 49160 | tf_op jit(solution)/shard_map/ppermute | solution.py:492
  8.5 1.6 %collective-permute-start.1 = (f32[64,128]{1,0:T(8,128)S(1)}, f32[64,128]{1,0:T(8,128)S(1)}, u32[]{:S(2)}, u32[]{:S(2)}) collective-permute-start(f32[64,128]{1,0:T(8,128)S(1)} %get-tuple-element.102.traces), channel_id=1, source_target_pairs={{0,4},{4,0},{8,12},{12,8},{1,5},{5,1},{9,13},{13,9},{2,6},{6,2},{1... | collective-permute-start | bytes 98312 | tf_op jit(solution)/shard_map/ppermute | solution.py:492
  12.2 1.7 %collective-permute-start.3 = (f32[64,128]{1,0:T(8,128)S(1)}, f32[64,128]{1,0:T(8,128)S(1)}, u32[]{:S(2)}, u32[]{:S(2)}) collective-permute-start(f32[64,128]{1,0:T(8,128)S(1)} %get-tuple-element.102.traces), channel_id=1, source_target_pairs={{0,12},{4,8},{8,4},{12,0},{1,13},{5,9},{9,5},{13,1},{2,14},{6,10},... | collective-permute-start | bytes 98312 | tf_op jit(solution)/shard_map/ppermute | solution.py:492
  13.9 4.0 %collective-permute-done.2 = f32[64,128]{1,0:T(8,128)S(1)} collective-permute-done((f32[64,128]{1,0:T(8,128)S(1)}, f32[64,128]{1,0:T(8,128)S(1)}, u32[]{:S(2)}, u32[]{:S(2)}) %collective-permute-start.2) | collective-permute-done | bytes 32800 | tf_op jit(solution)/shard_map/ppermute | solution.py:492
  17.9 2.8 %collective-permute-start.6 = (f32[256,128]{1,0:T(8,128)S(1)}, f32[256,128]{1,0:T(8,128)S(1)}, u32[]{:S(2)}, u32[]{:S(2)}) collective-permute-start(f32[256,128]{1,0:T(8,128)S(1)} %constant_dynamic-update-slice_fusion.2), channel_id=1, source_target_pairs={{0,96},{32,64},{64,32},{96,0},{1,97},{33,65},{65,33},{97,1},{2,98}... | collective-permute-start | bytes 393224 | tf_op jit(solution)/shard_map/ppermute | solution.py:492
  21.4 3.2 %first.1 = (bf16[64,256,128]{2,1,0:T(8,128)(2,1)S(1)}, f32[512,128]{1,0:T(8,128)S(1)}, f32[4,128,128]{2,1,0:T(8,128)S(1)}) custom-call(f32[8192,128]{1,0:T(8,128)} %movie.1, f32[512,128]{1,0:T(8,128)S(1)} %get-tuple-element.59.foot), custom_call_target="tpu_custom_call" | custom-call | flops 67108864 | bytes 1048576 | tf_op jit(solution)/shard_map/first/pallas_call | solution.py:172
  26.2 4.4 %collective-permute-start.7 = (f32[1024,128]{1,0:T(8,128)S(1)}, f32[1024,128]{1,0:T(8,128)S(1)}, u32[]{:S(2)}, u32[]{:S(2)}) collective-permute-start(f32[1024,128]{1,0:T(8,128)S(1)} %pad_maximum_fusion.near), channel_id=1, source_target_pairs={{0,16},{16,0},{1,17},{17,1},{2,18},{18,2},{3,19},{19,3},{4,20},{20... | collective-permute-start | bytes 1572872 | tf_op jit(solution)/shard_map/ppermute | solution.py:492
  35.7 1.8 %collective-permute-start.9 = (f32[264,128]{1,0:T(8,128)S(1)}, f32[264,128]{1,0:T(8,128)S(1)}, u32[]{:S(2)}, u32[]{:S(2)}) collective-permute-start(f32[264,128]{1,0:T(8,128)S(1)} %get-tuple-element.70), channel_id=1, source_target_pairs={{0,96},{32,64},{64,32},{96,0},{1,97},{33,65},{65,33},{97,1},{2,98}... | collective-permute-start | bytes 405512 | tf_op jit(solution)/shard_map/ppermute | solution.py:492
  39.1 3.1 %collective-permute-done.9.b = f32[264,128]{1,0:T(8,128)S(1)} collective-permute-done((f32[264,128]{1,0:T(8,128)S(1)}, f32[264,128]{1,0:T(8,128)S(1)}, u32[]{:S(2)}, u32[]{:S(2)}) %collective-permute-start.9) | collective-permute-done | bytes 135200 | tf_op jit(solution)/shard_map/ppermute | solution.py:492
  50.2 4.0 %collective-permute-start.15 = (f32[72,128]{1,0:T(8,128)S(1)}, f32[72,128]{1,0:T(8,128)S(1)}, u32[]{:S(2)}, u32[]{:S(2)}) collective-permute-start(f32[72,128]{1,0:T(8,128)S(1)} %fold_z.2.own), channel_id=1, source_target_pairs={{0,140},{4,136},{8,132},{12,128},{128,12},{132,8},{136,4},{140,0},... | collective-permute-start | bytes 110600 | tf_op jit(solution)/shard_map/ppermute | solution.py:492
  55.7 1.7 %collective-permute-start.18 = (f32[64,128]{1,0:T(8,128)S(1)}, f32[64,128]{1,0:T(8,128)S(1)}, u32[]{:S(2)}, u32[]{:S(2)}) collective-permute-start(f32[64,128]{1,0:T(8,128)S(1)} %update.2.traces), channel_id=1, source_target_pairs={{0,12},{4,8},{8,4},{12,0},{1,13},{5,9},{9,5},{13,1},{2,14},{6,10},... | collective-permute-start | bytes 98312 | tf_op jit(solution)/shard_map/ppermute | solution.py:492
  57.4 1.8 %collective-permute-start.17 = (f32[64,128]{1,0:T(8,128)S(1)}, f32[64,128]{1,0:T(8,128)S(1)}, u32[]{:S(2)}, u32[]{:S(2)}) collective-permute-start(f32[64,128]{1,0:T(8,128)S(1)} %update.2.traces), channel_id=1, source_target_pairs={{0,8},{4,12},{8,0},{12,4},{1,9},{5,13},{9,1},{13,5},{2,10},{6,14},... | collective-permute-start | bytes 98312 | tf_op jit(solution)/shard_map/ppermute | solution.py:492
  62.0 1.8 %collective-permute-start.21 = (f32[256,128]{1,0:T(8,128)S(1)}, f32[256,128]{1,0:T(8,128)S(1)}, u32[]{:S(2)}, u32[]{:S(2)}) collective-permute-start(f32[256,128]{1,0:T(8,128)S(1)} %pad_maximum_fusion.2), channel_id=1, source_target_pairs={{0,96},{32,64},{64,32},{96,0},{1,97},{33,65},{65,33},{97,1},{2,98}... | collective-permute-start | bytes 393224 | tf_op jit(solution)/shard_map/ppermute | solution.py:492
  65.4 3.8 %collective-permute-done.19 = f32[256,128]{1,0:T(8,128)S(1)} collective-permute-done((f32[256,128]{1,0:T(8,128)S(1)}, f32[256,128]{1,0:T(8,128)S(1)}, u32[]{:S(2)}, u32[]{:S(2)}) %collective-permute-start.19) | collective-permute-done | bytes 131104 | tf_op jit(solution)/shard_map/ppermute | solution.py:492
  69.2 6.8 %collective-permute-start.22 = (f32[1024,128]{1,0:T(8,128)S(1)}, f32[1024,128]{1,0:T(8,128)S(1)}, u32[]{:S(2)}, u32[]{:S(2)}) collective-permute-start(f32[1024,128]{1,0:T(8,128)S(1)} %constant_dynamic-update-slice_fusion.7.near), channel_id=1, source_target_pairs={{0,16},{16,0},{1,17},{17,1},{2,18},{18,2},{3,19},{19,3},{4,20},{20... | collective-permute-start | bytes 1572872 | tf_op jit(solution)/shard_map/ppermute | solution.py:492
  81.3 2.5 %collective-permute-start.24 = (f32[136,128]{1,0:T(8,128)S(1)}, f32[136,128]{1,0:T(8,128)S(1)}, u32[]{:S(2)}, u32[]{:S(2)}) collective-permute-start(f32[136,128]{1,0:T(8,128)S(1)} %gradient.8), channel_id=1, source_target_pairs={{0,2},{1,3},{2,0},{3,1},{4,6},{5,7},{6,4},{7,5},{8,10},{9,11},{10,... | collective-permute-start | bytes 208904 | tf_op jit(solution)/shard_map/ppermute | solution.py:492
  84.5 2.4 %collective-permute-done.24.c = f32[136,128]{1,0:T(8,128)S(1)} collective-permute-done((f32[136,128]{1,0:T(8,128)S(1)}, f32[136,128]{1,0:T(8,128)S(1)}, u32[]{:S(2)}, u32[]{:S(2)}) %collective-permute-start.24) | collective-permute-done | bytes 69664 | tf_op jit(solution)/shard_map/ppermute | solution.py:492
  86.9 1.6 collective-permute-done.25.d
  96.1 2.4 %collective-permute-start.29 = (f32[4,264,128]{2,1,0:T(8,128)S(1)}, f32[4,264,128]{2,1,0:T(8,128)S(1)}, u32[]{:S(2)}, u32[]{:S(2)}) collective-permute-start(f32[4,264,128]{2,1,0:T(8,128)S(1)} %get-tuple-element.91), channel_id=1, source_target_pairs={{0,16},{16,0},{1,17},{17,1},{2,18},{18,2},{3,19},{19,3},{4,20},{20... | collective-permute-start | bytes 1622024 | tf_op jit(solution)/shard_map/ppermute | solution.py:492
  100.1 1.8 %collective-permute-start.30 = (f32[264,128]{1,0:T(8,128)S(1)}, f32[264,128]{1,0:T(8,128)S(1)}, u32[]{:S(2)}, u32[]{:S(2)}) collective-permute-start(f32[264,128]{1,0:T(8,128)S(1)} %get-tuple-element.93), channel_id=1, source_target_pairs={{0,96},{32,64},{64,32},{96,0},{1,97},{33,65},{65,33},{97,1},{2,98}... | collective-permute-start | bytes 405512 | tf_op jit(solution)/shard_map/ppermute | solution.py:492
  103.5 3.1 %collective-permute-done.30.b = f32[264,128]{1,0:T(8,128)S(1)} collective-permute-done((f32[264,128]{1,0:T(8,128)S(1)}, f32[264,128]{1,0:T(8,128)S(1)}, u32[]{:S(2)}, u32[]{:S(2)}) %collective-permute-start.30) | collective-permute-done | bytes 135200 | tf_op jit(solution)/shard_map/ppermute | solution.py:492
  109.5 1.7 %collective-permute-start.33 = (f32[72,128]{1,0:T(8,128)S(1)}, f32[72,128]{1,0:T(8,128)S(1)}, u32[]{:S(2)}, u32[]{:S(2)}) collective-permute-start(f32[72,128]{1,0:T(8,128)S(1)} %get-tuple-element.97), channel_id=1, source_target_pairs={{0,8},{4,12},{8,0},{12,4},{1,9},{5,13},{9,1},{13,5},{2,10},{6,14},... | collective-permute-start | bytes 110600 | tf_op jit(solution)/shard_map/ppermute | solution.py:492
  111.2 1.6 %collective-permute-start.34 = (f32[72,128]{1,0:T(8,128)S(1)}, f32[72,128]{1,0:T(8,128)S(1)}, u32[]{:S(2)}, u32[]{:S(2)}) collective-permute-start(f32[72,128]{1,0:T(8,128)S(1)} %get-tuple-element.98), channel_id=1, source_target_pairs={{0,12},{4,8},{8,4},{12,0},{1,13},{5,9},{9,5},{13,1},{2,14},{6,10},... | collective-permute-start | bytes 110600 | tf_op jit(solution)/shard_map/ppermute | solution.py:492
  113.3 2.6 %collective-permute-done.34.c = f32[72,128]{1,0:T(8,128)S(1)} collective-permute-done((f32[72,128]{1,0:T(8,128)S(1)}, f32[72,128]{1,0:T(8,128)S(1)}, u32[]{:S(2)}, u32[]{:S(2)}) %collective-permute-start.34) | collective-permute-done | bytes 36896 | tf_op jit(solution)/shard_map/ppermute | solution.py:492
  116.0 3.0 %collective-permute-start.36 = (f32[72,128]{1,0:T(8,128)S(1)}, f32[72,128]{1,0:T(8,128)S(1)}, u32[]{:S(2)}, u32[]{:S(2)}) collective-permute-start(f32[72,128]{1,0:T(8,128)S(1)} %fold_z.3.own), channel_id=1, source_target_pairs={{0,140},{4,136},{8,132},{12,128},{128,12},{132,8},{136,4},{140,0},... | collective-permute-start | bytes 110600 | tf_op jit(solution)/shard_map/ppermute | solution.py:492
  120.5 2.2 %collective-permute-start.39 = (f32[64,128]{1,0:T(8,128)S(1)}, f32[64,128]{1,0:T(8,128)S(1)}, u32[]{:S(2)}, u32[]{:S(2)}) collective-permute-start(f32[64,128]{1,0:T(8,128)S(1)} %update.3), channel_id=1, source_target_pairs={{0,12},{4,8},{8,4},{12,0},{1,13},{5,9},{9,5},{13,1},{2,14},{6,10},... | collective-permute-start | bytes 98312 | tf_op jit(solution)/shard_map/ppermute | solution.py:492
  126.8 1.8 %collective-permute-start.42 = (f32[256,128]{1,0:T(8,128)S(1)}, f32[256,128]{1,0:T(8,128)S(1)}, u32[]{:S(2)}, u32[]{:S(2)}) collective-permute-start(f32[256,128]{1,0:T(8,128)S(1)} %pad_maximum_fusion.3), channel_id=1, source_target_pairs={{0,96},{32,64},{64,32},{96,0},{1,97},{33,65},{65,33},{97,1},{2,98}... | collective-permute-start | bytes 393224 | tf_op jit(solution)/shard_map/ppermute | solution.py:492
  130.1 3.8 %collective-permute-done.40 = f32[256,128]{1,0:T(8,128)S(1)} collective-permute-done((f32[256,128]{1,0:T(8,128)S(1)}, f32[256,128]{1,0:T(8,128)S(1)}, u32[]{:S(2)}, u32[]{:S(2)}) %collective-permute-start.40) | collective-permute-done | bytes 131104 | tf_op jit(solution)/shard_map/ppermute | solution.py:492
  134.0 6.5 %collective-permute-start.43 = (f32[1024,128]{1,0:T(8,128)S(1)}, f32[1024,128]{1,0:T(8,128)S(1)}, u32[]{:S(2)}, u32[]{:S(2)}) collective-permute-start(f32[1024,128]{1,0:T(8,128)S(1)} %constant_dynamic-update-slice_fusion.14.near), channel_id=1, source_target_pairs={{0,16},{16,0},{1,17},{17,1},{2,18},{18,2},{3,19},{19,3},{4,20},{20... | collective-permute-start | bytes 1572872 | tf_op jit(solution)/shard_map/ppermute | solution.py:492
  145.7 2.2 %collective-permute-start.45 = (f32[136,128]{1,0:T(8,128)S(1)}, f32[136,128]{1,0:T(8,128)S(1)}, u32[]{:S(2)}, u32[]{:S(2)}) collective-permute-start(f32[136,128]{1,0:T(8,128)S(1)} %gradient.11), channel_id=1, source_target_pairs={{0,2},{1,3},{2,0},{3,1},{4,6},{5,7},{6,4},{7,5},{8,10},{9,11},{10,... | collective-permute-start | bytes 208904 | tf_op jit(solution)/shard_map/ppermute | solution.py:492
  149.0 2.0 %collective-permute-done.45.c = f32[136,128]{1,0:T(8,128)S(1)} collective-permute-done((f32[136,128]{1,0:T(8,128)S(1)}, f32[136,128]{1,0:T(8,128)S(1)}, u32[]{:S(2)}, u32[]{:S(2)}) %collective-permute-start.45) | collective-permute-done | bytes 69664 | tf_op jit(solution)/shard_map/ppermute | solution.py:492
  151.0 1.6 collective-permute-done.46.d
  (126 shorter events, 66.4 us)
Async XLA Ops:
  0.6 7.8 %collective-permute-start = (f32[32,128]{1,0:T(8,128)}, f32[32,128]{1,0:T(8,128)S(1)}, u32[]{:S(2)}, u32[]{:S(2)}) collective-permute-start(f32[32,128]{1,0:T(8,128)} %param.5), channel_id=1, source_target_pairs={{0,140},{4,136},{8,132},{12,128},{128,12},{132,8},{136,4},{140,0},... | collective-permute-start | bytes 49160 | tf_op jit(solution)/shard_map/ppermute | solution.py:492
  8.5 5.5 %collective-permute-start.1 = (f32[64,128]{1,0:T(8,128)S(1)}, f32[64,128]{1,0:T(8,128)S(1)}, u32[]{:S(2)}, u32[]{:S(2)}) collective-permute-start(f32[64,128]{1,0:T(8,128)S(1)} %get-tuple-element.102.traces), channel_id=1, source_target_pairs={{0,4},{4,0},{8,12},{12,8},{1,5},{5,1},{9,13},{13,9},{2,6},{6,2},{1... | collective-permute-start | bytes 98312 | tf_op jit(solution)/shard_map/ppermute | solution.py:492
  12.2 5.7 %collective-permute-start.3 = (f32[64,128]{1,0:T(8,128)S(1)}, f32[64,128]{1,0:T(8,128)S(1)}, u32[]{:S(2)}, u32[]{:S(2)}) collective-permute-start(f32[64,128]{1,0:T(8,128)S(1)} %get-tuple-element.102.traces), channel_id=1, source_target_pairs={{0,12},{4,8},{8,4},{12,0},{1,13},{5,9},{9,5},{13,1},{2,14},{6,10},... | collective-permute-start | bytes 98312 | tf_op jit(solution)/shard_map/ppermute | solution.py:492
  17.9 6.8 %collective-permute-start.6 = (f32[256,128]{1,0:T(8,128)S(1)}, f32[256,128]{1,0:T(8,128)S(1)}, u32[]{:S(2)}, u32[]{:S(2)}) collective-permute-start(f32[256,128]{1,0:T(8,128)S(1)} %constant_dynamic-update-slice_fusion.2), channel_id=1, source_target_pairs={{0,96},{32,64},{64,32},{96,0},{1,97},{33,65},{65,33},{97,1},{2,98}... | collective-permute-start | bytes 393224 | tf_op jit(solution)/shard_map/ppermute | solution.py:492
  20.7 5.4 %collective-permute-start.5 = (f32[256,128]{1,0:T(8,128)S(1)}, f32[256,128]{1,0:T(8,128)S(1)}, u32[]{:S(2)}, u32[]{:S(2)}) collective-permute-start(f32[256,128]{1,0:T(8,128)S(1)} %constant_dynamic-update-slice_fusion.2), channel_id=1, source_target_pairs={{0,64},{32,96},{64,0},{96,32},{1,65},{33,97},{65,1},{97,33},{2,66}... | collective-permute-start | bytes 393224 | tf_op jit(solution)/shard_map/ppermute | solution.py:492
  21.1 5.1 %collective-permute-start.4 = (f32[256,128]{1,0:T(8,128)S(1)}, f32[256,128]{1,0:T(8,128)S(1)}, u32[]{:S(2)}, u32[]{:S(2)}) collective-permute-start(f32[256,128]{1,0:T(8,128)S(1)} %constant_dynamic-update-slice_fusion.2), channel_id=1, source_target_pairs={{0,32},{32,0},{64,96},{96,64},{1,33},{33,1},{65,97},{97,65},{2,34}... | collective-permute-start | bytes 393224 | tf_op jit(solution)/shard_map/ppermute | solution.py:492
  26.2 6.0 %collective-permute-start.7 = (f32[1024,128]{1,0:T(8,128)S(1)}, f32[1024,128]{1,0:T(8,128)S(1)}, u32[]{:S(2)}, u32[]{:S(2)}) collective-permute-start(f32[1024,128]{1,0:T(8,128)S(1)} %pad_maximum_fusion.near), channel_id=1, source_target_pairs={{0,16},{16,0},{1,17},{17,1},{2,18},{18,2},{3,19},{19,3},{4,20},{20... | collective-permute-start | bytes 1572872 | tf_op jit(solution)/shard_map/ppermute | solution.py:492
  35.7 6.4 %collective-permute-start.9 = (f32[264,128]{1,0:T(8,128)S(1)}, f32[264,128]{1,0:T(8,128)S(1)}, u32[]{:S(2)}, u32[]{:S(2)}) collective-permute-start(f32[264,128]{1,0:T(8,128)S(1)} %get-tuple-element.70), channel_id=1, source_target_pairs={{0,96},{32,64},{64,32},{96,0},{1,97},{33,65},{65,33},{97,1},{2,98}... | collective-permute-start | bytes 405512 | tf_op jit(solution)/shard_map/ppermute | solution.py:492
  37.5 6.1 %collective-permute-start.10 = (f32[264,128]{1,0:T(8,128)S(1)}, f32[264,128]{1,0:T(8,128)S(1)}, u32[]{:S(2)}, u32[]{:S(2)}) collective-permute-start(f32[264,128]{1,0:T(8,128)S(1)} %get-tuple-element.71), channel_id=1, source_target_pairs={{0,64},{32,96},{64,0},{96,32},{1,65},{33,97},{65,1},{97,33},{2,66}... | collective-permute-start | bytes 405512 | tf_op jit(solution)/shard_map/ppermute | solution.py:492
  37.9 7.2 %collective-permute-start.11 = (f32[264,128]{1,0:T(8,128)S(1)}, f32[264,128]{1,0:T(8,128)S(1)}, u32[]{:S(2)}, u32[]{:S(2)}) collective-permute-start(f32[264,128]{1,0:T(8,128)S(1)} %get-tuple-element.72), channel_id=1, source_target_pairs={{0,32},{32,0},{64,96},{96,64},{1,33},{33,1},{65,97},{97,65},{2,34}... | collective-permute-start | bytes 405512 | tf_op jit(solution)/shard_map/ppermute | solution.py:492
  45.3 4.9 %collective-permute-start.13 = (f32[72,128]{1,0:T(8,128)S(1)}, f32[72,128]{1,0:T(8,128)S(1)}, u32[]{:S(2)}, u32[]{:S(2)}) collective-permute-start(f32[72,128]{1,0:T(8,128)S(1)} %get-tuple-element.75), channel_id=1, source_target_pairs={{0,12},{4,8},{8,4},{12,0},{1,13},{5,9},{9,5},{13,1},{2,14},{6,10},... | collective-permute-start | bytes 110600 | tf_op jit(solution)/shard_map/ppermute | solution.py:492
  50.2 5.3 %collective-permute-start.15 = (f32[72,128]{1,0:T(8,128)S(1)}, f32[72,128]{1,0:T(8,128)S(1)}, u32[]{:S(2)}, u32[]{:S(2)}) collective-permute-start(f32[72,128]{1,0:T(8,128)S(1)} %fold_z.2.own), channel_id=1, source_target_pairs={{0,140},{4,136},{8,132},{12,128},{128,12},{132,8},{136,4},{140,0},... | collective-permute-start | bytes 110600 | tf_op jit(solution)/shard_map/ppermute | solution.py:492
  55.7 5.0 %collective-permute-start.18 = (f32[64,128]{1,0:T(8,128)S(1)}, f32[64,128]{1,0:T(8,128)S(1)}, u32[]{:S(2)}, u32[]{:S(2)}) collective-permute-start(f32[64,128]{1,0:T(8,128)S(1)} %update.2.traces), channel_id=1, source_target_pairs={{0,12},{4,8},{8,4},{12,0},{1,13},{5,9},{9,5},{13,1},{2,14},{6,10},... | collective-permute-start | bytes 98312 | tf_op jit(solution)/shard_map/ppermute | solution.py:492
  62.0 7.2 %collective-permute-start.21 = (f32[256,128]{1,0:T(8,128)S(1)}, f32[256,128]{1,0:T(8,128)S(1)}, u32[]{:S(2)}, u32[]{:S(2)}) collective-permute-start(f32[256,128]{1,0:T(8,128)S(1)} %pad_maximum_fusion.2), channel_id=1, source_target_pairs={{0,96},{32,64},{64,32},{96,0},{1,97},{33,65},{65,33},{97,1},{2,98}... | collective-permute-start | bytes 393224 | tf_op jit(solution)/shard_map/ppermute | solution.py:492
  63.8 5.4 %collective-permute-start.20 = (f32[256,128]{1,0:T(8,128)S(1)}, f32[256,128]{1,0:T(8,128)S(1)}, u32[]{:S(2)}, u32[]{:S(2)}) collective-permute-start(f32[256,128]{1,0:T(8,128)S(1)} %pad_maximum_fusion.2), channel_id=1, source_target_pairs={{0,64},{32,96},{64,0},{96,32},{1,65},{33,97},{65,1},{97,33},{2,66}... | collective-permute-start | bytes 393224 | tf_op jit(solution)/shard_map/ppermute | solution.py:492
  64.1 5.0 %collective-permute-start.19 = (f32[256,128]{1,0:T(8,128)S(1)}, f32[256,128]{1,0:T(8,128)S(1)}, u32[]{:S(2)}, u32[]{:S(2)}) collective-permute-start(f32[256,128]{1,0:T(8,128)S(1)} %pad_maximum_fusion.2), channel_id=1, source_target_pairs={{0,32},{32,0},{64,96},{96,64},{1,33},{33,1},{65,97},{97,65},{2,34}... | collective-permute-start | bytes 393224 | tf_op jit(solution)/shard_map/ppermute | solution.py:492
  69.2 8.3 %collective-permute-start.22 = (f32[1024,128]{1,0:T(8,128)S(1)}, f32[1024,128]{1,0:T(8,128)S(1)}, u32[]{:S(2)}, u32[]{:S(2)}) collective-permute-start(f32[1024,128]{1,0:T(8,128)S(1)} %constant_dynamic-update-slice_fusion.7.near), channel_id=1, source_target_pairs={{0,16},{16,0},{1,17},{17,1},{2,18},{18,2},{3,19},{19,3},{4,20},{20... | collective-permute-start | bytes 1572872 | tf_op jit(solution)/shard_map/ppermute | solution.py:492
  81.3 5.5 %collective-permute-start.24 = (f32[136,128]{1,0:T(8,128)S(1)}, f32[136,128]{1,0:T(8,128)S(1)}, u32[]{:S(2)}, u32[]{:S(2)}) collective-permute-start(f32[136,128]{1,0:T(8,128)S(1)} %gradient.8), channel_id=1, source_target_pairs={{0,2},{1,3},{2,0},{3,1},{4,6},{5,7},{6,4},{7,5},{8,10},{9,11},{10,... | collective-permute-start | bytes 208904 | tf_op jit(solution)/shard_map/ppermute | solution.py:492
  83.8 4.7 %collective-permute-start.25 = (f32[136,128]{1,0:T(8,128)S(1)}, f32[136,128]{1,0:T(8,128)S(1)}, u32[]{:S(2)}, u32[]{:S(2)}) collective-permute-start(f32[136,128]{1,0:T(8,128)S(1)} %get-tuple-element.79), channel_id=1, source_target_pairs={{0,3},{1,2},{2,1},{3,0},{4,7},{5,6},{6,5},{7,4},{8,11},{9,10},{10,... | collective-permute-start | bytes 208904 | tf_op jit(solution)/shard_map/ppermute | solution.py:492
  90.1 4.6 %collective-permute-start.27 = (f32[128,128]{1,0:T(8,128)S(1)}, f32[128,128]{1,0:T(8,128)S(1)}, u32[]{:S(2)}, u32[]{:S(2)}) collective-permute-start(f32[128,128]{1,0:T(8,128)S(1)} %step.2.foot), channel_id=1, source_target_pairs={{0,2},{1,3},{2,0},{3,1},{4,6},{5,7},{6,4},{7,5},{8,10},{9,11},{10,... | collective-permute-start | bytes 196616 | tf_op jit(solution)/shard_map/ppermute | solution.py:492
  100.1 6.4 %collective-permute-start.30 = (f32[264,128]{1,0:T(8,128)S(1)}, f32[264,128]{1,0:T(8,128)S(1)}, u32[]{:S(2)}, u32[]{:S(2)}) collective-permute-start(f32[264,128]{1,0:T(8,128)S(1)} %get-tuple-element.93), channel_id=1, source_target_pairs={{0,96},{32,64},{64,32},{96,0},{1,97},{33,65},{65,33},{97,1},{2,98}... | collective-permute-start | bytes 405512 | tf_op jit(solution)/shard_map/ppermute | solution.py:492
  101.9 6.1 %collective-permute-start.31 = (f32[264,128]{1,0:T(8,128)S(1)}, f32[264,128]{1,0:T(8,128)S(1)}, u32[]{:S(2)}, u32[]{:S(2)}) collective-permute-start(f32[264,128]{1,0:T(8,128)S(1)} %get-tuple-element.94), channel_id=1, source_target_pairs={{0,64},{32,96},{64,0},{96,32},{1,65},{33,97},{65,1},{97,33},{2,66}... | collective-permute-start | bytes 405512 | tf_op jit(solution)/shard_map/ppermute | solution.py:492
  102.3 7.1 %collective-permute-start.32 = (f32[264,128]{1,0:T(8,128)S(1)}, f32[264,128]{1,0:T(8,128)S(1)}, u32[]{:S(2)}, u32[]{:S(2)}) collective-permute-start(f32[264,128]{1,0:T(8,128)S(1)} %get-tuple-element.95), channel_id=1, source_target_pairs={{0,32},{32,0},{64,96},{96,64},{1,33},{33,1},{65,97},{97,65},{2,34}... | collective-permute-start | bytes 405512 | tf_op jit(solution)/shard_map/ppermute | solution.py:492
  111.2 4.7 %collective-permute-start.34 = (f32[72,128]{1,0:T(8,128)S(1)}, f32[72,128]{1,0:T(8,128)S(1)}, u32[]{:S(2)}, u32[]{:S(2)}) collective-permute-start(f32[72,128]{1,0:T(8,128)S(1)} %get-tuple-element.98), channel_id=1, source_target_pairs={{0,12},{4,8},{8,4},{12,0},{1,13},{5,9},{9,5},{13,1},{2,14},{6,10},... | collective-permute-start | bytes 110600 | tf_op jit(solution)/shard_map/ppermute | solution.py:492
  120.5 4.8 %collective-permute-start.39 = (f32[64,128]{1,0:T(8,128)S(1)}, f32[64,128]{1,0:T(8,128)S(1)}, u32[]{:S(2)}, u32[]{:S(2)}) collective-permute-start(f32[64,128]{1,0:T(8,128)S(1)} %update.3), channel_id=1, source_target_pairs={{0,12},{4,8},{8,4},{12,0},{1,13},{5,9},{9,5},{13,1},{2,14},{6,10},... | collective-permute-start | bytes 98312 | tf_op jit(solution)/shard_map/ppermute | solution.py:492
  126.8 7.2 %collective-permute-start.42 = (f32[256,128]{1,0:T(8,128)S(1)}, f32[256,128]{1,0:T(8,128)S(1)}, u32[]{:S(2)}, u32[]{:S(2)}) collective-permute-start(f32[256,128]{1,0:T(8,128)S(1)} %pad_maximum_fusion.3), channel_id=1, source_target_pairs={{0,96},{32,64},{64,32},{96,0},{1,97},{33,65},{65,33},{97,1},{2,98}... | collective-permute-start | bytes 393224 | tf_op jit(solution)/shard_map/ppermute | solution.py:492
  128.5 5.4 %collective-permute-start.41 = (f32[256,128]{1,0:T(8,128)S(1)}, f32[256,128]{1,0:T(8,128)S(1)}, u32[]{:S(2)}, u32[]{:S(2)}) collective-permute-start(f32[256,128]{1,0:T(8,128)S(1)} %pad_maximum_fusion.3), channel_id=1, source_target_pairs={{0,64},{32,96},{64,0},{96,32},{1,65},{33,97},{65,1},{97,33},{2,66}... | collective-permute-start | bytes 393224 | tf_op jit(solution)/shard_map/ppermute | solution.py:492
  129.0 4.9 %collective-permute-start.40 = (f32[256,128]{1,0:T(8,128)S(1)}, f32[256,128]{1,0:T(8,128)S(1)}, u32[]{:S(2)}, u32[]{:S(2)}) collective-permute-start(f32[256,128]{1,0:T(8,128)S(1)} %pad_maximum_fusion.3), channel_id=1, source_target_pairs={{0,32},{32,0},{64,96},{96,64},{1,33},{33,1},{65,97},{97,65},{2,34}... | collective-permute-start | bytes 393224 | tf_op jit(solution)/shard_map/ppermute | solution.py:492
  134.0 8.1 %collective-permute-start.43 = (f32[1024,128]{1,0:T(8,128)S(1)}, f32[1024,128]{1,0:T(8,128)S(1)}, u32[]{:S(2)}, u32[]{:S(2)}) collective-permute-start(f32[1024,128]{1,0:T(8,128)S(1)} %constant_dynamic-update-slice_fusion.14.near), channel_id=1, source_target_pairs={{0,16},{16,0},{1,17},{17,1},{2,18},{18,2},{3,19},{19,3},{4,20},{20... | collective-permute-start | bytes 1572872 | tf_op jit(solution)/shard_map/ppermute | solution.py:492
  145.7 5.3 %collective-permute-start.45 = (f32[136,128]{1,0:T(8,128)S(1)}, f32[136,128]{1,0:T(8,128)S(1)}, u32[]{:S(2)}, u32[]{:S(2)}) collective-permute-start(f32[136,128]{1,0:T(8,128)S(1)} %gradient.11), channel_id=1, source_target_pairs={{0,2},{1,3},{2,0},{3,1},{4,6},{5,7},{6,4},{7,5},{8,10},{9,11},{10,... | collective-permute-start | bytes 208904 | tf_op jit(solution)/shard_map/ppermute | solution.py:492
  147.9 4.7 %collective-permute-start.46 = (f32[136,128]{1,0:T(8,128)S(1)}, f32[136,128]{1,0:T(8,128)S(1)}, u32[]{:S(2)}, u32[]{:S(2)}) collective-permute-start(f32[136,128]{1,0:T(8,128)S(1)} %get-tuple-element.101), channel_id=1, source_target_pairs={{0,3},{1,2},{2,1},{3,0},{4,7},{5,6},{6,5},{7,4},{8,11},{9,10},{10,... | collective-permute-start | bytes 208904 | tf_op jit(solution)/shard_map/ppermute | solution.py:492
  153.5 4.6 %collective-permute-start.48 = (f32[128,128]{1,0:T(8,128)S(1)}, f32[128,128]{1,0:T(8,128)S(1)}, u32[]{:S(2)}, u32[]{:S(2)}) collective-permute-start(f32[128,128]{1,0:T(8,128)S(1)} %step.3.f0), channel_id=1, source_target_pairs={{0,2},{1,3},{2,0},{3,1},{4,6},{5,7},{6,4},{7,5},{8,10},{9,11},{10,... | collective-permute-start | bytes 196616 | tf_op jit(solution)/shard_map/ppermute | solution.py:492
  (18 other events, 67.3 us)
